TPU v7x, 512 devices: a whole 4x8x8 slice. The times are simulated.
512 devices in a mesh: section: 8 (over z_hi, x), dp: 64 (over z_lo, y, core).
Axes of the slice: x: 4, y: 8, z: 8 (z_hi: 2, z_lo: 4; z = z_hi * 4 + z_lo), core: 2. Of those that a mesh axis runs over, the one named last changes fastest.
Arguments:
- inputs: bfloat16 [8192, 8192], P('dp', 'section'), may hold values from -6 to 6
- cotangent: bfloat16 [8192, 8192], P('dp', 'section'), may hold values from -6 to 6
- weights: bfloat16 [8, 64, 8192], P('section'), may hold values from -0.0625 to 0.0625
- momentum: bfloat16 [8, 64, 64, 8192], P('section', 'dp'), may hold values from -6 to 6
- keep_index: int32 [8, 64, 128, 32], P('section', 'dp'), may hold values from 0 to 4095, as said below
Outputs:
- momentum_out: bfloat16 [8, 64, 64, 8192], P('section', 'dp')
- update: bfloat16 [8, 64, 64, 8192], P('section', 'dp')
Inputs may be any that keep to these rules, and one draw needn't show every extreme that they name: `keep_index`: the 32 positions of one block of one replica and layer are all different.
All inputs are finite; a program needn't handle non-finite values.
Results may differ from a plain program's by a relative error of at most 0.0095.
Values may be sent and summed in bfloat16 or wider, within the bound.
No kernel may reach another device: no remote copies, remote signals or barrier semaphores. Data moves between devices by JAX's collectives and lax.ppermute only.
A program may use at most 64 MiB of HBM per device.

v0:
```python
import math

import jax
import jax.numpy as jnp
from jax import lax
from jax.sharding import PartitionSpec as P

MICRO = 8


DECAY = 0.999


def in_one_piece(arrays, axis, dim, along):
    ends, at = ([], 0)
    for a in arrays[:-1]:
        at += a.shape[along]
        ends.append(at)
    both = jnp.concatenate(arrays, axis=along)
    return tuple(jnp.split(lax.all_gather(both, axis, axis=dim, tiled=True), ends, axis=along))


def from_behind(value, axis, steps):
    count = lax.axis_size(axis)
    leading, last = (max(0, -steps), min(count, count - steps))
    return lax.ppermute(value, axis, [(source, source + steps) for source in range(leading, last)])


def dct_basis(length):
    freq = jnp.arange(length, dtype=jnp.float32)[:, None]
    position = jnp.arange(length, dtype=jnp.float32)[None, :]
    dct_table = jnp.cos(math.pi * (position + 0.5) * freq / length) * math.sqrt(2.0 / length)
    return jnp.where(freq == 0, dct_table * math.sqrt(0.5), dct_table)


def forward_groups(field_in, dct_table):
    row_count, columns = field_in.shape
    blocks = field_in.reshape(row_count // 64, 64, columns // 64, 64)
    coeffs = jnp.einsum(
        "kn,anbm,jm->akbj", dct_table, blocks, dct_table, precision=lax.Precision.HIGHEST
    )
    return coeffs.reshape(-1)


def inverse_groups(flat_in, dct_table, row_count, columns):
    blocks = flat_in.reshape(row_count // 64, 64, columns // 64, 64)
    field_out = jnp.einsum(
        "kn,akbj,jm->anbm", dct_table, blocks, dct_table, precision=lax.Precision.HIGHEST
    )
    return field_out.reshape(row_count, columns)


def group_offsets(position, col_groups):
    group_id = jnp.arange(position.shape[0], dtype=jnp.int32)[:, None]
    return (
        group_id // col_groups * (4096 * col_groups)
        + position // 64 * (64 * col_groups)
        + group_id % col_groups * 64
        + position % 64
    )


def silu_slope(pre_act):
    sigma_h = jax.nn.sigmoid(pre_act)
    return sigma_h * (1.0 + pre_act * (1.0 - sigma_h))


def store_slot(saved, value, slot_clip, is_valid):
    previous = lax.dynamic_index_in_dim(saved, slot_clip, 0, keepdims=False)
    return lax.dynamic_update_index_in_dim(
        saved, jnp.where(is_valid, value, previous), slot_clip, 0
    )


def local(inputs, cotangent, weights, momentum, keep_index):
    sections = lax.axis_size("section")
    section_index = lax.axis_index("section")
    whole_inputs, whole_grads = in_one_piece((inputs, cotangent), "section", 1, 0)
    weight = weights[0]
    row_count, columns = weight.shape
    tok_dev = whole_inputs.shape[0]
    tok_mb = tok_dev // MICRO
    tick_count = MICRO + sections - 1
    first_in = whole_inputs.reshape(MICRO, tok_mb, columns)
    last_grad = whole_grads.reshape(MICRO, tok_mb, columns)

    def forward_tick(tick_idx, loop_state):
        incoming, saved_x, saved_a, saved_h = loop_state
        micro_slot = tick_idx - section_index
        is_valid = (micro_slot >= 0) & (micro_slot < MICRO)
        slot_clip = jnp.clip(micro_slot, 0, MICRO - 1)
        own_first = lax.dynamic_index_in_dim(first_in, slot_clip, 0, keepdims=False)
        activation = jnp.where(section_index == 0, own_first, incoming)
        pre_act = jnp.einsum("td,cd->tc", activation, weight, preferred_element_type=jnp.float32)
        gated_act = jax.nn.silu(pre_act).astype(jnp.bfloat16)
        result = (
            activation.astype(jnp.float32)
            + jnp.einsum("tc,cd->td", gated_act, weight, preferred_element_type=jnp.float32)
        ).astype(jnp.bfloat16)
        saved_x = store_slot(saved_x, activation, slot_clip, is_valid)
        saved_a = store_slot(saved_a, gated_act, slot_clip, is_valid)
        saved_h = store_slot(saved_h, pre_act, slot_clip, is_valid)
        outgoing = from_behind(result, "section", 1)
        return (outgoing, saved_x, saved_a, saved_h)

    start_state = (
        jnp.zeros((tok_mb, columns), jnp.bfloat16),
        jnp.zeros((MICRO, tok_mb, columns), jnp.bfloat16),
        jnp.zeros((MICRO, tok_mb, row_count), jnp.bfloat16),
        jnp.zeros((MICRO, tok_mb, row_count), jnp.float32),
    )
    loop_state = lax.fori_loop(0, tick_count, forward_tick, start_state)
    saved_x, saved_a, saved_h = (loop_state[1], loop_state[2], loop_state[3])

    def backward_tick(tick_idx, loop_state):
        incoming, saved_g, saved_d = loop_state
        micro_slot = tick_idx - (sections - 1 - section_index)
        is_valid = (micro_slot >= 0) & (micro_slot < MICRO)
        slot_clip = jnp.clip(micro_slot, 0, MICRO - 1)
        own_last = lax.dynamic_index_in_dim(last_grad, slot_clip, 0, keepdims=False)
        grad_in = jnp.where(section_index == sections - 1, own_last, incoming)
        pre_act = lax.dynamic_index_in_dim(saved_h, slot_clip, 0, keepdims=False)
        errors = jnp.einsum("td,cd->tc", grad_in, weight, preferred_element_type=jnp.float32)
        deltas = (errors * silu_slope(pre_act)).astype(jnp.bfloat16)
        saved_g = store_slot(saved_g, grad_in, slot_clip, is_valid)
        saved_d = store_slot(saved_d, deltas, slot_clip, is_valid)
        sent_back = (
            grad_in.astype(jnp.float32)
            + jnp.einsum("tc,cd->td", deltas, weight, preferred_element_type=jnp.float32)
        ).astype(jnp.bfloat16)
        outgoing = from_behind(sent_back, "section", -1)
        return (outgoing, saved_g, saved_d)

    back_state = (
        jnp.zeros((tok_mb, columns), jnp.bfloat16),
        jnp.zeros((MICRO, tok_mb, columns), jnp.bfloat16),
        jnp.zeros((MICRO, tok_mb, row_count), jnp.bfloat16),
    )
    back_out = lax.fori_loop(0, tick_count, backward_tick, back_state)
    saved_g = back_out[1].reshape(tok_dev, columns)
    saved_d = back_out[2].reshape(tok_dev, row_count)
    grad_total = jnp.einsum(
        "tc,td->cd",
        saved_a.reshape(tok_dev, row_count),
        saved_g,
        preferred_element_type=jnp.float32,
    )
    grad_total = grad_total + jnp.einsum(
        "tc,td->cd", saved_d, saved_x.reshape(tok_dev, columns), preferred_element_type=jnp.float32
    )
    dct_table = dct_basis(64)
    momentum_new = DECAY * momentum[0, 0].astype(jnp.float32) + grad_total
    coeffs = forward_groups(momentum_new, dct_table)
    offsets = group_offsets(keep_index[0, 0], columns // 64)
    kept_values = coeffs[offsets]
    own_sparse = jnp.zeros_like(coeffs).at[offsets.reshape(-1)].add(kept_values.reshape(-1))
    own_field = inverse_groups(own_sparse, dct_table, row_count, columns)
    momentum_out = (momentum_new - own_field).astype(jnp.bfloat16)
    update = lax.psum(own_field, "dp")
    return (momentum_out[None, None], update.astype(jnp.bfloat16)[None, None])


def solution(mesh):
    return jax.shard_map(
        local,
        mesh=mesh,
        in_specs=(
            P("dp", "section"),
            P("dp", "section"),
            P("section", None, None),
            P("section", "dp", None, None),
            P("section", "dp", None, None),
        ),
        out_specs=(P("section", "dp", None, None), P("section", "dp", None, None)),
        check_vma=False,
    )
```

profile of v0, /device:TPU:6, one launch (start us, length us, event | category | flops | bytes accessed | tf_op | source)
XLA Modules:
  0.0 1089.6 jit_solution(4277291674360943587)
XLA Ops:
  12.5 115.1 %all-gather.2.cloned.1.call-done = bf16[256,8192]{1,0:T(8,128)(2,1)} async-done(((bf16[256,1024]{1,0:T(8,128)(2,1)}), bf16[256,8192]{1,0:T(8,128)(2,1)}) %all-gather.2.cloned.1.call-update) | async-done | bytes 4194320 | tf_op jit(solution)/shard_map/all_gather | solution.py:20
  133.6 264.2 %while.39 = (s32[]{:T(128)}, bf16[16,8192]{1,0:T(8,128)(2,1)}, bf16[8,16,8192]{2,1,0:T(8,128)(2,1)S(1)}, bf16[8,16,64]{2,1,0:T(8,128)(2,1)S(1)}, f32[8,16,64]{2,...) while((s32[]{:T(128)}, bf16[16,8192]{1,0:T(8,128)(2,1)}, ...), condition=%wide.region_1.2_spmd, body=%wide.region_0.1_spmd.sunk | while | flops 34222088 | bytes 6873366 | solution.py:112
  164.4 10.3 collective-permute-start
  182.1 10.3 collective-permute-start
  199.9 10.3 collective-permute-start
  217.7 10.3 collective-permute-start
  253.2 10.3 collective-permute-start
  271.0 10.4 collective-permute-start
  288.9 10.4 collective-permute-start
  306.7 10.4 collective-permute-start
  324.6 10.3 collective-permute-start
  362.1 10.3 collective-permute-start
  382.5 10.4 collective-permute-start
  400.8 303.0 %while.40 = (s32[]{:T(128)}, bf16[16,8192]{1,0:T(8,128)(2,1)}, bf16[8,16,8192]{2,1,0:T(8,128)(2,1)}, bf16[8,16,64]{2,1,0:T(8,128)(2,1)}, pred[]{:T(512)}, /*inde...) while((s32[]{:T(128)}, bf16[16,8192]{1,0:T(8,128)(2,1)}, ...), condition=%wide.region_3.4_spmd, body=%wide.region_2.3_spmd.sunk | while | flops 34220040 | bytes 6834956 | solution.py:139
  407.5 15.6 %collective-permute-done.1 = bf16[16,8192]{1,0:T(8,128)(2,1)S(1)} collective-permute-done((bf16[16,8192]{1,0:T(8,128)(2,1)S(1)}, bf16[16,8192]{1,0:T(8,128)(2,1)S(1)}, u32[]{:S(2)}, u32[]{:S(2)}) %collective-permute-start.1) | collective-permute-done | bytes 262176 | tf_op jit(solution)/shard_map/while/body/eval_jaxpr/ppermute | solution.py:26
  430.5 14.3 %collective-permute-done.1 = bf16[16,8192]{1,0:T(8,128)(2,1)S(1)} collective-permute-done((bf16[16,8192]{1,0:T(8,128)(2,1)S(1)}, bf16[16,8192]{1,0:T(8,128)(2,1)S(1)}, u32[]{:S(2)}, u32[]{:S(2)}) %collective-permute-start.1) | collective-permute-done | bytes 262176 | tf_op jit(solution)/shard_map/while/body/eval_jaxpr/ppermute | solution.py:26
  452.2 13.3 %collective-permute-done.1 = bf16[16,8192]{1,0:T(8,128)(2,1)S(1)} collective-permute-done((bf16[16,8192]{1,0:T(8,128)(2,1)S(1)}, bf16[16,8192]{1,0:T(8,128)(2,1)S(1)}, u32[]{:S(2)}, u32[]{:S(2)}) %collective-permute-start.1) | collective-permute-done | bytes 262176 | tf_op jit(solution)/shard_map/while/body/eval_jaxpr/ppermute | solution.py:26
  472.8 12.4 %collective-permute-done.1 = bf16[16,8192]{1,0:T(8,128)(2,1)S(1)} collective-permute-done((bf16[16,8192]{1,0:T(8,128)(2,1)S(1)}, bf16[16,8192]{1,0:T(8,128)(2,1)S(1)}, u32[]{:S(2)}, u32[]{:S(2)}) %collective-permute-start.1) | collective-permute-done | bytes 262176 | tf_op jit(solution)/shard_map/while/body/eval_jaxpr/ppermute | solution.py:26
  492.6 12.4 %collective-permute-done.1 = bf16[16,8192]{1,0:T(8,128)(2,1)S(1)} collective-permute-done((bf16[16,8192]{1,0:T(8,128)(2,1)S(1)}, bf16[16,8192]{1,0:T(8,128)(2,1)S(1)}, u32[]{:S(2)}, u32[]{:S(2)}) %collective-permute-start.1) | collective-permute-done | bytes 262176 | tf_op jit(solution)/shard_map/while/body/eval_jaxpr/ppermute | solution.py:26
  512.4 12.4 %collective-permute-done.1 = bf16[16,8192]{1,0:T(8,128)(2,1)S(1)} collective-permute-done((bf16[16,8192]{1,0:T(8,128)(2,1)S(1)}, bf16[16,8192]{1,0:T(8,128)(2,1)S(1)}, u32[]{:S(2)}, u32[]{:S(2)}) %collective-permute-start.1) | collective-permute-done | bytes 262176 | tf_op jit(solution)/shard_map/while/body/eval_jaxpr/ppermute | solution.py:26
  532.3 12.4 %collective-permute-done.1 = bf16[16,8192]{1,0:T(8,128)(2,1)S(1)} collective-permute-done((bf16[16,8192]{1,0:T(8,128)(2,1)S(1)}, bf16[16,8192]{1,0:T(8,128)(2,1)S(1)}, u32[]{:S(2)}, u32[]{:S(2)}) %collective-permute-start.1) | collective-permute-done | bytes 262176 | tf_op jit(solution)/shard_map/while/body/eval_jaxpr/ppermute | solution.py:26
  552.1 12.4 %collective-permute-done.1 = bf16[16,8192]{1,0:T(8,128)(2,1)S(1)} collective-permute-done((bf16[16,8192]{1,0:T(8,128)(2,1)S(1)}, bf16[16,8192]{1,0:T(8,128)(2,1)S(1)}, u32[]{:S(2)}, u32[]{:S(2)}) %collective-permute-start.1) | collective-permute-done | bytes 262176 | tf_op jit(solution)/shard_map/while/body/eval_jaxpr/ppermute | solution.py:26
  571.9 12.4 %collective-permute-done.1 = bf16[16,8192]{1,0:T(8,128)(2,1)S(1)} collective-permute-done((bf16[16,8192]{1,0:T(8,128)(2,1)S(1)}, bf16[16,8192]{1,0:T(8,128)(2,1)S(1)}, u32[]{:S(2)}, u32[]{:S(2)}) %collective-permute-start.1) | collective-permute-done | bytes 262176 | tf_op jit(solution)/shard_map/while/body/eval_jaxpr/ppermute | solution.py:26
  591.8 12.4 %collective-permute-done.1 = bf16[16,8192]{1,0:T(8,128)(2,1)S(1)} collective-permute-done((bf16[16,8192]{1,0:T(8,128)(2,1)S(1)}, bf16[16,8192]{1,0:T(8,128)(2,1)S(1)}, u32[]{:S(2)}, u32[]{:S(2)}) %collective-permute-start.1) | collective-permute-done | bytes 262176 | tf_op jit(solution)/shard_map/while/body/eval_jaxpr/ppermute | solution.py:26
  611.6 12.4 %collective-permute-done.1 = bf16[16,8192]{1,0:T(8,128)(2,1)S(1)} collective-permute-done((bf16[16,8192]{1,0:T(8,128)(2,1)S(1)}, bf16[16,8192]{1,0:T(8,128)(2,1)S(1)}, u32[]{:S(2)}, u32[]{:S(2)}) %collective-permute-start.1) | collective-permute-done | bytes 262176 | tf_op jit(solution)/shard_map/while/body/eval_jaxpr/ppermute | solution.py:26
  631.4 12.4 %collective-permute-done.1 = bf16[16,8192]{1,0:T(8,128)(2,1)S(1)} collective-permute-done((bf16[16,8192]{1,0:T(8,128)(2,1)S(1)}, bf16[16,8192]{1,0:T(8,128)(2,1)S(1)}, u32[]{:S(2)}, u32[]{:S(2)}) %collective-permute-start.1) | collective-permute-done | bytes 262176 | tf_op jit(solution)/shard_map/while/body/eval_jaxpr/ppermute | solution.py:26
  651.2 12.4 %collective-permute-done.1 = bf16[16,8192]{1,0:T(8,128)(2,1)S(1)} collective-permute-done((bf16[16,8192]{1,0:T(8,128)(2,1)S(1)}, bf16[16,8192]{1,0:T(8,128)(2,1)S(1)}, u32[]{:S(2)}, u32[]{:S(2)}) %collective-permute-start.1) | collective-permute-done | bytes 262176 | tf_op jit(solution)/shard_map/while/body/eval_jaxpr/ppermute | solution.py:26
  671.1 12.4 %collective-permute-done.1 = bf16[16,8192]{1,0:T(8,128)(2,1)S(1)} collective-permute-done((bf16[16,8192]{1,0:T(8,128)(2,1)S(1)}, bf16[16,8192]{1,0:T(8,128)(2,1)S(1)}, u32[]{:S(2)}, u32[]{:S(2)}) %collective-permute-start.1) | collective-permute-done | bytes 262176 | tf_op jit(solution)/shard_map/while/body/eval_jaxpr/ppermute | solution.py:26
  690.8 12.4 %collective-permute-done.1 = bf16[16,8192]{1,0:T(8,128)(2,1)S(1)} collective-permute-done((bf16[16,8192]{1,0:T(8,128)(2,1)S(1)}, bf16[16,8192]{1,0:T(8,128)(2,1)S(1)}, u32[]{:S(2)}, u32[]{:S(2)}) %collective-permute-start.1) | collective-permute-done | bytes 262176 | tf_op jit(solution)/shard_map/while/body/eval_jaxpr/ppermute | solution.py:26
  727.7 23.0 %gather_fusion = f32[4096]{0:T(1024)S(1)} fusion(f32[524288]{0:T(1024)S(1)} %reshape.407, s32[4096]{0:T(1024)S(1)} %broadcast_clamp_fusion), kind=kCustom, calls=%fused_computation | custom fusion | bytes 49152 | tf_op jit(solution)/shard_map/gather | solution.py:155
  750.8 22.6 %scatter_custom_fusion = f32[524288]{0:T(1024)S(1)} fusion(s32[4096]{0:T(1024)S(1)} %bitcast.169, f32[4096]{0:T(1024)S(1)} %gather_fusion, f32[]{:T(128)} %constant.209.clone.1), kind=kCustom, calls=%fused_computation.46 | custom fusion | flops 4096 | bytes 2097156 | tf_op jit(solution)/shard_map/scatter-add | solution.py:156
  795.4 287.4 %all-reduce.1 = bf16[64,8192]{1,0:T(8,128)(2,1)} all-reduce(f32[64,8192]{1,0:T(8,128)} %reshape.410), channel_id=1, replica_groups=mesh['section'=8,'dp'=64] {'dp'}, use_global_device_ids=true, to_apply=%region_5.6 | all-reduce | flops 524288 | bytes 3145728 | tf_op jit(solution)/shard_map/psum | solution.py:159
  (332 shorter events, 320.3 us)
Async XLA Ops:
  7.2 120.4 %all-gather.2.cloned.1.call-start = ((), (), s32[]{:S(2)}) async-start(), calls=%async_computation | async-start | bytes 4718592 | tf_op jit(solution)/shard_map/all_gather | solution.py:20
  136.1 9.1 collective-permute-start
  148.6 12.5 %collective-permute-start = (bf16[16,8192]{1,0:T(8,128)(2,1)}, bf16[16,8192]{1,0:T(8,128)(2,1)S(1)}, u32[]{:S(2)}, u32[]{:S(2)}) collective-permute-start(bf16[16,8192]{1,0:T(8,128)(2,1)} %fusion.99), channel_id=1, source_target_pairs={{0,64},{64,128},{128,192},{192,256},{256,320},{320,384},{384,448},... | collective-permute-start | bytes 786440 | tf_op jit(solution)/shard_map/while/body/eval_jaxpr/ppermute | solution.py:26
  164.4 14.5 %collective-permute-start = (bf16[16,8192]{1,0:T(8,128)(2,1)}, bf16[16,8192]{1,0:T(8,128)(2,1)S(1)}, u32[]{:S(2)}, u32[]{:S(2)}) collective-permute-start(bf16[16,8192]{1,0:T(8,128)(2,1)} %fusion.99), channel_id=1, source_target_pairs={{0,64},{64,128},{128,192},{192,256},{256,320},{320,384},{384,448},... | collective-permute-start | bytes 786440 | tf_op jit(solution)/shard_map/while/body/eval_jaxpr/ppermute | solution.py:26
  182.1 14.5 %collective-permute-start = (bf16[16,8192]{1,0:T(8,128)(2,1)}, bf16[16,8192]{1,0:T(8,128)(2,1)S(1)}, u32[]{:S(2)}, u32[]{:S(2)}) collective-permute-start(bf16[16,8192]{1,0:T(8,128)(2,1)} %fusion.99), channel_id=1, source_target_pairs={{0,64},{64,128},{128,192},{192,256},{256,320},{320,384},{384,448},... | collective-permute-start | bytes 786440 | tf_op jit(solution)/shard_map/while/body/eval_jaxpr/ppermute | solution.py:26
  199.9 14.5 %collective-permute-start = (bf16[16,8192]{1,0:T(8,128)(2,1)}, bf16[16,8192]{1,0:T(8,128)(2,1)S(1)}, u32[]{:S(2)}, u32[]{:S(2)}) collective-permute-start(bf16[16,8192]{1,0:T(8,128)(2,1)} %fusion.99), channel_id=1, source_target_pairs={{0,64},{64,128},{128,192},{192,256},{256,320},{320,384},{384,448},... | collective-permute-start | bytes 786440 | tf_op jit(solution)/shard_map/while/body/eval_jaxpr/ppermute | solution.py:26
  217.7 14.5 %collective-permute-start = (bf16[16,8192]{1,0:T(8,128)(2,1)}, bf16[16,8192]{1,0:T(8,128)(2,1)S(1)}, u32[]{:S(2)}, u32[]{:S(2)}) collective-permute-start(bf16[16,8192]{1,0:T(8,128)(2,1)} %fusion.99), channel_id=1, source_target_pairs={{0,64},{64,128},{128,192},{192,256},{256,320},{320,384},{384,448},... | collective-permute-start | bytes 786440 | tf_op jit(solution)/shard_map/while/body/eval_jaxpr/ppermute | solution.py:26
  235.4 14.5 %collective-permute-start = (bf16[16,8192]{1,0:T(8,128)(2,1)}, bf16[16,8192]{1,0:T(8,128)(2,1)S(1)}, u32[]{:S(2)}, u32[]{:S(2)}) collective-permute-start(bf16[16,8192]{1,0:T(8,128)(2,1)} %fusion.99), channel_id=1, source_target_pairs={{0,64},{64,128},{128,192},{192,256},{256,320},{320,384},{384,448},... | collective-permute-start | bytes 786440 | tf_op jit(solution)/shard_map/while/body/eval_jaxpr/ppermute | solution.py:26
  253.2 14.5 %collective-permute-start = (bf16[16,8192]{1,0:T(8,128)(2,1)}, bf16[16,8192]{1,0:T(8,128)(2,1)S(1)}, u32[]{:S(2)}, u32[]{:S(2)}) collective-permute-start(bf16[16,8192]{1,0:T(8,128)(2,1)} %fusion.99), channel_id=1, source_target_pairs={{0,64},{64,128},{128,192},{192,256},{256,320},{320,384},{384,448},... | collective-permute-start | bytes 786440 | tf_op jit(solution)/shard_map/while/body/eval_jaxpr/ppermute | solution.py:26
  271.0 14.6 %collective-permute-start = (bf16[16,8192]{1,0:T(8,128)(2,1)}, bf16[16,8192]{1,0:T(8,128)(2,1)S(1)}, u32[]{:S(2)}, u32[]{:S(2)}) collective-permute-start(bf16[16,8192]{1,0:T(8,128)(2,1)} %fusion.99), channel_id=1, source_target_pairs={{0,64},{64,128},{128,192},{192,256},{256,320},{320,384},{384,448},... | collective-permute-start | bytes 786440 | tf_op jit(solution)/shard_map/while/body/eval_jaxpr/ppermute | solution.py:26
  288.9 14.6 %collective-permute-start = (bf16[16,8192]{1,0:T(8,128)(2,1)}, bf16[16,8192]{1,0:T(8,128)(2,1)S(1)}, u32[]{:S(2)}, u32[]{:S(2)}) collective-permute-start(bf16[16,8192]{1,0:T(8,128)(2,1)} %fusion.99), channel_id=1, source_target_pairs={{0,64},{64,128},{128,192},{192,256},{256,320},{320,384},{384,448},... | collective-permute-start | bytes 786440 | tf_op jit(solution)/shard_map/while/body/eval_jaxpr/ppermute | solution.py:26
  306.7 14.6 %collective-permute-start = (bf16[16,8192]{1,0:T(8,128)(2,1)}, bf16[16,8192]{1,0:T(8,128)(2,1)S(1)}, u32[]{:S(2)}, u32[]{:S(2)}) collective-permute-start(bf16[16,8192]{1,0:T(8,128)(2,1)} %fusion.99), channel_id=1, source_target_pairs={{0,64},{64,128},{128,192},{192,256},{256,320},{320,384},{384,448},... | collective-permute-start | bytes 786440 | tf_op jit(solution)/shard_map/while/body/eval_jaxpr/ppermute | solution.py:26
  324.6 14.9 %collective-permute-start = (bf16[16,8192]{1,0:T(8,128)(2,1)}, bf16[16,8192]{1,0:T(8,128)(2,1)S(1)}, u32[]{:S(2)}, u32[]{:S(2)}) collective-permute-start(bf16[16,8192]{1,0:T(8,128)(2,1)} %fusion.99), channel_id=1, source_target_pairs={{0,64},{64,128},{128,192},{192,256},{256,320},{320,384},{384,448},... | collective-permute-start | bytes 786440 | tf_op jit(solution)/shard_map/while/body/eval_jaxpr/ppermute | solution.py:26
  342.8 16.0 %collective-permute-start = (bf16[16,8192]{1,0:T(8,128)(2,1)}, bf16[16,8192]{1,0:T(8,128)(2,1)S(1)}, u32[]{:S(2)}, u32[]{:S(2)}) collective-permute-start(bf16[16,8192]{1,0:T(8,128)(2,1)} %fusion.99), channel_id=1, source_target_pairs={{0,64},{64,128},{128,192},{192,256},{256,320},{320,384},{384,448},... | collective-permute-start | bytes 786440 | tf_op jit(solution)/shard_map/while/body/eval_jaxpr/ppermute | solution.py:26
  362.1 17.1 %collective-permute-start = (bf16[16,8192]{1,0:T(8,128)(2,1)}, bf16[16,8192]{1,0:T(8,128)(2,1)S(1)}, u32[]{:S(2)}, u32[]{:S(2)}) collective-permute-start(bf16[16,8192]{1,0:T(8,128)(2,1)} %fusion.99), channel_id=1, source_target_pairs={{0,64},{64,128},{128,192},{192,256},{256,320},{320,384},{384,448},... | collective-permute-start | bytes 786440 | tf_op jit(solution)/shard_map/while/body/eval_jaxpr/ppermute | solution.py:26
  382.5 14.6 %collective-permute-start = (bf16[16,8192]{1,0:T(8,128)(2,1)}, bf16[16,8192]{1,0:T(8,128)(2,1)S(1)}, u32[]{:S(2)}, u32[]{:S(2)}) collective-permute-start(bf16[16,8192]{1,0:T(8,128)(2,1)} %fusion.99), channel_id=1, source_target_pairs={{0,64},{64,128},{128,192},{192,256},{256,320},{320,384},{384,448},... | collective-permute-start | bytes 786440 | tf_op jit(solution)/shard_map/while/body/eval_jaxpr/ppermute | solution.py:26
  405.5 17.6 %collective-permute-start.1 = (bf16[16,8192]{1,0:T(8,128)(2,1)S(1)}, bf16[16,8192]{1,0:T(8,128)(2,1)S(1)}, u32[]{:S(2)}, u32[]{:S(2)}) collective-permute-start(bf16[16,8192]{1,0:T(8,128)(2,1)S(1)} %fusion.104), channel_id=1, source_target_pairs={{64,0},{128,64},{192,128},{256,192},{320,256},{384,320},{448,384},... | collective-permute-start | bytes 786440 | tf_op jit(solution)/shard_map/while/body/eval_jaxpr/ppermute | solution.py:26
  428.6 16.2 %collective-permute-start.1 = (bf16[16,8192]{1,0:T(8,128)(2,1)S(1)}, bf16[16,8192]{1,0:T(8,128)(2,1)S(1)}, u32[]{:S(2)}, u32[]{:S(2)}) collective-permute-start(bf16[16,8192]{1,0:T(8,128)(2,1)S(1)} %fusion.104), channel_id=1, source_target_pairs={{64,0},{128,64},{192,128},{256,192},{320,256},{384,320},{448,384},... | collective-permute-start | bytes 786440 | tf_op jit(solution)/shard_map/while/body/eval_jaxpr/ppermute | solution.py:26
  450.3 15.2 %collective-permute-start.1 = (bf16[16,8192]{1,0:T(8,128)(2,1)S(1)}, bf16[16,8192]{1,0:T(8,128)(2,1)S(1)}, u32[]{:S(2)}, u32[]{:S(2)}) collective-permute-start(bf16[16,8192]{1,0:T(8,128)(2,1)S(1)} %fusion.104), channel_id=1, source_target_pairs={{64,0},{128,64},{192,128},{256,192},{320,256},{384,320},{448,384},... | collective-permute-start | bytes 786440 | tf_op jit(solution)/shard_map/while/body/eval_jaxpr/ppermute | solution.py:26
  470.9 14.3 %collective-permute-start.1 = (bf16[16,8192]{1,0:T(8,128)(2,1)S(1)}, bf16[16,8192]{1,0:T(8,128)(2,1)S(1)}, u32[]{:S(2)}, u32[]{:S(2)}) collective-permute-start(bf16[16,8192]{1,0:T(8,128)(2,1)S(1)} %fusion.104), channel_id=1, source_target_pairs={{64,0},{128,64},{192,128},{256,192},{320,256},{384,320},{448,384},... | collective-permute-start | bytes 786440 | tf_op jit(solution)/shard_map/while/body/eval_jaxpr/ppermute | solution.py:26
  490.7 14.3 %collective-permute-start.1 = (bf16[16,8192]{1,0:T(8,128)(2,1)S(1)}, bf16[16,8192]{1,0:T(8,128)(2,1)S(1)}, u32[]{:S(2)}, u32[]{:S(2)}) collective-permute-start(bf16[16,8192]{1,0:T(8,128)(2,1)S(1)} %fusion.104), channel_id=1, source_target_pairs={{64,0},{128,64},{192,128},{256,192},{320,256},{384,320},{448,384},... | collective-permute-start | bytes 786440 | tf_op jit(solution)/shard_map/while/body/eval_jaxpr/ppermute | solution.py:26
  510.5 14.4 %collective-permute-start.1 = (bf16[16,8192]{1,0:T(8,128)(2,1)S(1)}, bf16[16,8192]{1,0:T(8,128)(2,1)S(1)}, u32[]{:S(2)}, u32[]{:S(2)}) collective-permute-start(bf16[16,8192]{1,0:T(8,128)(2,1)S(1)} %fusion.104), channel_id=1, source_target_pairs={{64,0},{128,64},{192,128},{256,192},{320,256},{384,320},{448,384},... | collective-permute-start | bytes 786440 | tf_op jit(solution)/shard_map/while/body/eval_jaxpr/ppermute | solution.py:26
  530.3 14.4 %collective-permute-start.1 = (bf16[16,8192]{1,0:T(8,128)(2,1)S(1)}, bf16[16,8192]{1,0:T(8,128)(2,1)S(1)}, u32[]{:S(2)}, u32[]{:S(2)}) collective-permute-start(bf16[16,8192]{1,0:T(8,128)(2,1)S(1)} %fusion.104), channel_id=1, source_target_pairs={{64,0},{128,64},{192,128},{256,192},{320,256},{384,320},{448,384},... | collective-permute-start | bytes 786440 | tf_op jit(solution)/shard_map/while/body/eval_jaxpr/ppermute | solution.py:26
  550.2 14.4 %collective-permute-start.1 = (bf16[16,8192]{1,0:T(8,128)(2,1)S(1)}, bf16[16,8192]{1,0:T(8,128)(2,1)S(1)}, u32[]{:S(2)}, u32[]{:S(2)}) collective-permute-start(bf16[16,8192]{1,0:T(8,128)(2,1)S(1)} %fusion.104), channel_id=1, source_target_pairs={{64,0},{128,64},{192,128},{256,192},{320,256},{384,320},{448,384},... | collective-permute-start | bytes 786440 | tf_op jit(solution)/shard_map/while/body/eval_jaxpr/ppermute | solution.py:26
  570.0 14.4 %collective-permute-start.1 = (bf16[16,8192]{1,0:T(8,128)(2,1)S(1)}, bf16[16,8192]{1,0:T(8,128)(2,1)S(1)}, u32[]{:S(2)}, u32[]{:S(2)}) collective-permute-start(bf16[16,8192]{1,0:T(8,128)(2,1)S(1)} %fusion.104), channel_id=1, source_target_pairs={{64,0},{128,64},{192,128},{256,192},{320,256},{384,320},{448,384},... | collective-permute-start | bytes 786440 | tf_op jit(solution)/shard_map/while/body/eval_jaxpr/ppermute | solution.py:26
  589.8 14.4 %collective-permute-start.1 = (bf16[16,8192]{1,0:T(8,128)(2,1)S(1)}, bf16[16,8192]{1,0:T(8,128)(2,1)S(1)}, u32[]{:S(2)}, u32[]{:S(2)}) collective-permute-start(bf16[16,8192]{1,0:T(8,128)(2,1)S(1)} %fusion.104), channel_id=1, source_target_pairs={{64,0},{128,64},{192,128},{256,192},{320,256},{384,320},{448,384},... | collective-permute-start | bytes 786440 | tf_op jit(solution)/shard_map/while/body/eval_jaxpr/ppermute | solution.py:26
  609.7 14.4 %collective-permute-start.1 = (bf16[16,8192]{1,0:T(8,128)(2,1)S(1)}, bf16[16,8192]{1,0:T(8,128)(2,1)S(1)}, u32[]{:S(2)}, u32[]{:S(2)}) collective-permute-start(bf16[16,8192]{1,0:T(8,128)(2,1)S(1)} %fusion.104), channel_id=1, source_target_pairs={{64,0},{128,64},{192,128},{256,192},{320,256},{384,320},{448,384},... | collective-permute-start | bytes 786440 | tf_op jit(solution)/shard_map/while/body/eval_jaxpr/ppermute | solution.py:26
  629.5 14.4 %collective-permute-start.1 = (bf16[16,8192]{1,0:T(8,128)(2,1)S(1)}, bf16[16,8192]{1,0:T(8,128)(2,1)S(1)}, u32[]{:S(2)}, u32[]{:S(2)}) collective-permute-start(bf16[16,8192]{1,0:T(8,128)(2,1)S(1)} %fusion.104), channel_id=1, source_target_pairs={{64,0},{128,64},{192,128},{256,192},{320,256},{384,320},{448,384},... | collective-permute-start | bytes 786440 | tf_op jit(solution)/shard_map/while/body/eval_jaxpr/ppermute | solution.py:26
  649.3 14.4 %collective-permute-start.1 = (bf16[16,8192]{1,0:T(8,128)(2,1)S(1)}, bf16[16,8192]{1,0:T(8,128)(2,1)S(1)}, u32[]{:S(2)}, u32[]{:S(2)}) collective-permute-start(bf16[16,8192]{1,0:T(8,128)(2,1)S(1)} %fusion.104), channel_id=1, source_target_pairs={{64,0},{128,64},{192,128},{256,192},{320,256},{384,320},{448,384},... | collective-permute-start | bytes 786440 | tf_op jit(solution)/shard_map/while/body/eval_jaxpr/ppermute | solution.py:26
  669.1 14.3 %collective-permute-start.1 = (bf16[16,8192]{1,0:T(8,128)(2,1)S(1)}, bf16[16,8192]{1,0:T(8,128)(2,1)S(1)}, u32[]{:S(2)}, u32[]{:S(2)}) collective-permute-start(bf16[16,8192]{1,0:T(8,128)(2,1)S(1)} %fusion.104), channel_id=1, source_target_pairs={{64,0},{128,64},{192,128},{256,192},{320,256},{384,320},{448,384},... | collective-permute-start | bytes 786440 | tf_op jit(solution)/shard_map/while/body/eval_jaxpr/ppermute | solution.py:26
  688.8 14.3 %collective-permute-start.1 = (bf16[16,8192]{1,0:T(8,128)(2,1)S(1)}, bf16[16,8192]{1,0:T(8,128)(2,1)S(1)}, u32[]{:S(2)}, u32[]{:S(2)}) collective-permute-start(bf16[16,8192]{1,0:T(8,128)(2,1)S(1)} %fusion.104), channel_id=1, source_target_pairs={{64,0},{128,64},{192,128},{256,192},{320,256},{384,320},{448,384},... | collective-permute-start | bytes 786440 | tf_op jit(solution)/shard_map/while/body/eval_jaxpr/ppermute | solution.py:26
  787.6 5.0 copy-start.2
  (38 other events, 44.1 us)
Sparse Core Ops, SparseCore 0:
  11.8 115.7 all-gather.1
where the time goes:
time: 1090 us
  waiting for transfers between devices  377 us (35%)
  blocking collectives  287 us (26%)
  starting transfers between devices  173 us (16%)
  local copies, waits for them, and re-layouts  107 us (10%)
  other arithmetic  74 us (7%)
  matrix products  55.4 us (5%)
  between operations  14.2 us (1%)
    psum x1, blocking collectives, local(): update = lax.psum(own_field, 'dp')  287 us
    ppermute x30, waiting for transfers between devices, from_behind(): lax.ppermute(value, axis, [(source, source + steps) for source in range(l...  262 us
    ppermute x30, starting transfers between devices, from_behind(): lax.ppermute(value, axis, [(source, source + steps) for source in range(l...  173 us
    all_gather x1, waiting for transfers between devices, in_one_piece(): lax.all_gather(both, axis, axis=dim, tiled=True)  115 us
    dynamic_update_slice x45, other arithmetic, store_slot(): lax.dynamic_update_index_in_dim(saved, jnp.where(is_valid, value, previou...  44.9 us
    dynamic_slice x75, local copies, waits for them, and re-layouts, store_slot(): previous = lax.dynamic_index_in_dim(saved, slot_clip, 0, keepdims=False)  25.5 us
    gather x1, local copies, waits for them, and re-layouts, local(): kept_values = coeffs[offsets]  23 us
    scatter-add x1, other arithmetic, local(): jnp.zeros_like(coeffs).at[offsets.reshape(-1)].add(kept_values.reshape(-1))  22.6 us
  transfers between devices with their start and end apart: 31, of which 31 were waited for; matrix products, arithmetic and copies ran while one was open for 0% of the time, Pallas kernels for 0%

commit v1 on v0

v1 whole, which is shorter than its diff:
```python
import math

import jax
import jax.numpy as jnp
from jax import lax
from jax.sharding import Mesh, PartitionSpec as P

DECAY = 0.999
S = ("zh", "x")
CHIP = ("zl", "y")
DP = ("zl", "y", "core")
F32 = jnp.float32
BF = jnp.bfloat16


def a2a(value, axis):
    return lax.all_to_all(value, axis, 0, 0, tiled=True)


def swap_cores(value):
    return lax.ppermute(value, "core", [(0, 1), (1, 0)])


def mm(a, b, dims):
    return lax.dot_general(a, b, (dims, ((), ())), preferred_element_type=F32)


def split(value):
    high = value.astype(BF)
    return high, (value - high.astype(F32)).astype(BF)


def dct_basis(length):
    freq = jnp.arange(length, dtype=F32)[:, None]
    position = jnp.arange(length, dtype=F32)[None, :]
    table = jnp.cos(math.pi * (position + 0.5) * freq / length) * math.sqrt(2.0 / length)
    return jnp.where(freq == 0, table * math.sqrt(0.5), table)


def silu_slope(h):
    s = jax.nn.sigmoid(h)
    return s * (1.0 + h * (1.0 - s))


def local(inputs, cotangent, weights, momentum, keep_index):
    ns = lax.axis_size(S)
    nd = lax.axis_size(DP)
    core = lax.axis_index("core")
    weight = weights[0]
    rows, width = weight.shape
    cols = width // ns
    tok = inputs.shape[0]
    part = tok // ns
    full = ns * rows
    groups = width // 64
    own = groups // nd

    half = lax.dynamic_slice_in_dim(weight, core * (rows // 2), rows // 2, 0)
    mine = a2a(half.reshape(rows // 2, ns, cols).transpose(1, 0, 2), S)
    other = swap_cores(mine)
    w = jnp.concatenate(
        [jnp.where(core == 0, mine, other), jnp.where(core == 0, other, mine)], axis=1
    ).reshape(full, cols)

    both = jnp.concatenate([inputs, cotangent], axis=0)
    proj = mm(both, w, ((1,), (1,))).astype(BF)
    gram = mm(w, w, ((1,), (1,))).astype(BF)
    packed = []
    for k in range(ns // 2):
        m = ns - 1 - k
        packed.append(
            jnp.concatenate(
                [
                    gram[m * rows : (m + 1) * rows, (m + 1) * rows :],
                    gram[k * rows : (k + 1) * rows, k * rows :],
                ],
                axis=1,
            )
        )
    packed = jnp.concatenate(packed, axis=0).reshape(ns, -1, full)
    payload = jnp.concatenate(
        [proj.reshape(2, ns, part, full).transpose(1, 0, 2, 3).reshape(ns, 2 * part, full), packed], axis=1
    )
    got = jnp.sum(a2a(payload, S).astype(F32), axis=0).astype(BF)
    got = a2a(jnp.broadcast_to(got[None], (ns,) + got.shape), S)
    h0 = got[:, :part].reshape(tok, full).astype(F32)
    e0 = got[:, part : 2 * part].reshape(tok, full).astype(F32)
    packed = got[:, 2 * part :].reshape(-1, full)

    def g_block(k, l):
        if k < ns // 2:
            return packed[k * rows : (k + 1) * rows, l * rows : (l + 1) * rows]
        m = ns - 1 - k
        at = (l - k - 1) * rows
        return packed[m * rows : (m + 1) * rows, at : at + rows]

    hs, acts, deltas = [], [], [None] * ns
    for l in range(ns):
        h = h0[:, l * rows : (l + 1) * rows]
        for k in range(l):
            h = h + mm(acts[k], g_block(k, l), ((1,), (0,)))
        hs.append(h)
        acts.append(jax.nn.silu(h).astype(BF))
    for l in reversed(range(ns)):
        e = e0[:, l * rows : (l + 1) * rows]
        for k in range(l + 1, ns):
            e = e + mm(deltas[k], g_block(l, k), ((1,), (1,)))
        deltas[l] = (e * silu_slope(hs[l])).astype(BF)
    act = jnp.concatenate(acts, axis=1)
    delta = jnp.concatenate(deltas, axis=1)

    cross = mm(act, delta, ((0,), (0,)))
    layer = jnp.arange(full) // rows
    upper = jnp.where(layer[:, None] < layer[None, :], cross, 0.0)
    cross_hi, cross_lo = split(upper + upper.T)
    grads = (
        mm(act, cotangent, ((0,), (0,)))
        + mm(delta, inputs, ((0,), (0,)))
        + mm(cross_hi, w, ((1,), (0,)))
        + mm(cross_lo, w, ((1,), (0,)))
    )
    grad = a2a(grads.astype(BF).reshape(ns, rows, cols), S).transpose(1, 0, 2).reshape(rows, width)

    table = dct_basis(64)
    fresh = DECAY * momentum[0, 0].astype(F32) + grad.astype(F32)
    blocks = fresh.reshape(rows, groups, 64)
    coef = jnp.einsum("kn,nbm,jm->bkj", table, blocks, table, precision=lax.Precision.HIGH)
    keep = keep_index[0, 0]
    lanes = jnp.arange(64, dtype=jnp.int32)
    row_hot = keep[:, :, None] // 64 == lanes
    col_hot = keep[:, :, None] % 64 == lanes
    mask = jnp.einsum("bik,bij->bkj", row_hot.astype(BF), col_hot.astype(BF), preferred_element_type=F32)
    picked = jnp.einsum("bik,bkj->bij", row_hot.astype(F32), coef, precision=lax.Precision.HIGH)
    values = jnp.sum(jnp.where(col_hot, picked, 0.0), axis=2)
    own_field = jnp.einsum("kn,bkj,jm->nbm", table, coef * mask, table, precision=lax.Precision.HIGH)
    momentum_out = (fresh - own_field.reshape(rows, width)).astype(BF)

    sent = jnp.concatenate([values.reshape(nd, -1), keep.astype(F32).reshape(nd, -1)], axis=1)
    seen = a2a(sent, DP)
    n = own * keep.shape[1]
    val = seen[:, :n].reshape(nd, own, -1).transpose(1, 0, 2).reshape(own, -1)
    pos = seen[:, n:].astype(jnp.int32).reshape(nd, own, -1).transpose(1, 0, 2).reshape(own, -1)
    val_hi, val_lo = split(val)
    row_hot = pos[:, :, None] // 64 == lanes
    col_hot = (pos[:, :, None] % 64 == lanes).astype(BF)
    summed = sum(
        jnp.einsum(
            "bik,bij->bkj", jnp.where(row_hot, v[:, :, None], 0).astype(BF), col_hot, preferred_element_type=F32
        )
        for v in (val_hi, val_lo)
    )
    decoded = jnp.einsum("kn,bkj,jm->nbm", table, summed, table, precision=lax.Precision.HIGH)
    decoded = decoded.reshape(64, own * 64).astype(BF)
    nc = nd // 2
    here = a2a(jnp.broadcast_to(decoded[None], (nc,) + decoded.shape), CHIP)
    there = swap_cores(here)
    update = jnp.stack([jnp.where(core == 0, here, there), jnp.where(core == 0, there, here)], axis=1)
    update = update.transpose(2, 0, 1, 3).reshape(rows, width)
    return (momentum_out[None, None], update[None, None])


def solution(mesh):
    fine = Mesh(mesh.devices.reshape(2, mesh.shape["section"] // 2, mesh.shape["dp"] // 16, 8, 2), ("zh", "x", "zl", "y", "core"))
    return jax.shard_map(
        local,
        mesh=fine,
        in_specs=(
            P(DP, S),
            P(DP, S),
            P(S, None, None),
            P(S, DP, None, None),
            P(S, DP, None, None),
        ),
        out_specs=(P(S, DP, None, None), P(S, DP, None, None)),
        check_vma=False,
    )
```

time: 1090 us -> 217 us (0.20)
  waiting for transfers between devices: 377 us -> 15.3 us
  blocking collectives: 287 us -> 74.9 us
  starting transfers between devices: 173 us -> 27.3 us
  local copies, waits for them, and re-layouts: 107 us -> 40.2 us
  other arithmetic: 74 us -> 13 us
  between operations: 14.2 us -> 1.31 us
  matrix products: 55.4 us -> 43 us
    psum x1 -> x0, blocking collectives: 287 us -> none  [local(): update = lax.psum(own_field, 'dp')]
    ppermute x30 -> x2, waiting for transfers between devices: 262 us -> 1.87 us  [swap_cores(): return lax.ppermute(value, 'core', [(0, 1), (1, 0)])]
    ppermute x30 -> x2, starting transfers between devices: 173 us -> 3.82 us  [swap_cores(): return lax.ppermute(value, 'core', [(0, 1), (1, 0)])]
    all_gather x1 -> x0, waiting for transfers between devices: 115 us -> none  [in_one_piece(): lax.all_gather(both, axis, axis=dim, tiled=True)]
    all_to_all x0 -> x3, blocking collectives: none -> 74.9 us  [a2a(): return lax.all_to_all(value, axis, 0, 0, tiled=True)]
    dynamic_update_slice x45 -> x0, other arithmetic: 44.9 us -> none  [store_slot(): lax.dynamic_update_index_in_dim(saved, jnp.where(is_valid, value, previou...]
    dynamic_slice x75 -> x1, local copies, waits for them, and re-layouts: 25.5 us -> 0.03 us  [local(): half = lax.dynamic_slice_in_dim(weight, core * (rows // 2), rows // 2, 0)]
    all_to_all x0 -> x3, starting transfers between devices: none -> 23.5 us  [a2a(): return lax.all_to_all(value, axis, 0, 0, tiled=True)]
  transfers between devices with their start and end apart: 31 -> 5, of which waited for: 31 -> 3; matrix products, arithmetic and copies ran while one was open for 0% -> 14% of each run, Pallas kernels for 0% -> 0%
where the time goes in v1:
time: 217 us; the launch traced here: 215 us
  blocking collectives  74.9 us (35%)
  matrix products  43 us (20%)
  local copies, waits for them, and re-layouts  40.2 us (19%)
  starting transfers between devices  27.3 us (13%)
  waiting for transfers between devices  15.3 us (7%)
  other arithmetic  13 us (6%)
    all_to_all x3, blocking collectives, a2a(): return lax.all_to_all(value, axis, 0, 0, tiled=True)  74.9 us
    all_to_all x3, starting transfers between devices, a2a(): return lax.all_to_all(value, axis, 0, 0, tiled=True)  23.5 us
    dot_general x63, matrix products, mm(): return lax.dot_general(a, b, (dims, ((), ())), preferred_element_type=F32)  19 us
    all_to_all x3, waiting for transfers between devices, a2a(): return lax.all_to_all(value, axis, 0, 0, tiled=True)  13.4 us
    dot_general x2, matrix products, local(): jnp.einsum('kn,nbm,jm->bkj', table, blocks, table, precision=lax.Precisio...  7.2 us
    add x1, other arithmetic, local(): fresh = DECAY * momentum[0, 0].astype(F32) + grad.astype(F32)  6.51 us
    dot_general x2, matrix products, local(): jnp.einsum('kn,bkj,jm->nbm', table, coef * mask, table, precision=lax.Pre...  6.04 us
    dot_general x1, local copies, waits for them, and re-layouts, local(): jnp.einsum('kn,nbm,jm->bkj', table, blocks, table, precision=lax.Precisio...  5.57 us
  transfers between devices with their start and end apart: 5, of which 3 were waited for; matrix products, arithmetic and copies ran while one was open for 14% of the time, Pallas kernels for 0%

profile of v1, /device:TPU:6, one launch (start us, length us, event | category | flops | bytes accessed | tf_op | source)
XLA Modules:
  0.0 215.0 jit_solution(10437381771532113040)
XLA Ops:
  2.5 24.6 %all_to_all.37 = bf16[8,32,1024]{2,1,0:T(8,128)(2,1)S(1)} all-to-all(bf16[8,32,1024]{2,1,0:T(8,128)(2,1)S(1)} %copy.84), channel_id=1, replica_groups=mesh['zh'=2,'x'=4,'zl'=4,'y'=8,'core'=2] {'zh','x'}, dimensions={0} | all-to-all | bytes 1048576 | tf_op jit(solution)/shard_map/all_to_all | solution.py:17
  27.1 1.9 collective-permute-start
  29.1 1.9 collective-permute-done
  32.9 20.5 %all_to_all.38 = bf16[8,64,512]{2,1,0:T(8,128)(2,1)S(1)} all-to-all(bf16[8,64,512]{2,1,0:T(8,128)(2,1)S(1)} %pad_maximum_fusion.1), channel_id=1, replica_groups=mesh['zh'=2,'x'=4,'zl'=4,'y'=8,'core'=2] {'zh','x'}, dimensions={0} | all-to-all | bytes 1048576 | tf_op jit(solution)/shard_map/all_to_all | solution.py:17
  54.3 9.3 %all-to-all-start.2 = ((bf16[8,64,512]{2,1,0:T(8,128)(2,1)}), bf16[8,64,512]{2,1,0:T(8,128)(2,1)S(1)}, u32[]{:S(2)}, u32[]{:S(2)}) async-start(bf16[8,64,512]{2,1,0:T(8,128)(2,1)} %broadcast_in_dim.67), calls=%async_computation.2 | async-start | bytes 1048576 | tf_op jit(solution)/shard_map/all_to_all | solution.py:17
  63.7 10.1 %all-to-all-done.2 = bf16[8,64,512]{2,1,0:T(8,128)(2,1)S(1)} async-done(((bf16[8,64,512]{2,1,0:T(8,128)(2,1)}), bf16[8,64,512]{2,1,0:T(8,128)(2,1)S(1)}, u32[]{:S(2)}, u32[]{:S(2)}) %all-to-all-start.2) | async-done | bytes 524320 | tf_op jit(solution)/shard_map/all_to_all | solution.py:17
  86.9 1.7 fusion.179
  88.9 1.8 fusion.178
  93.3 1.8 add_convert_fusion
  95.1 9.5 %all-to-all-start.3 = ((bf16[8,64,1024]{2,1,0:T(8,128)(2,1)}), bf16[8,64,1024]{2,1,0:T(8,128)(2,1)S(1)}, u32[]{:S(2)}, u32[]{:S(2)}) async-start(bf16[8,64,1024]{2,1,0:T(8,128)(2,1)} %bitcast.170), calls=%async_computation.3 | async-start | bytes 2097152 | tf_op jit(solution)/shard_map/all_to_all | solution.py:17
  104.6 1.4 convert_multiply_fusion
  106.1 3.0 %mul.245 = f32[64,128,64]{2,1,0:T(8,128)} reshape(f32[1,1,64,8192]{3,2,1,0:T(8,128)S(1)} %convert_multiply_fusion) | data formatting | bytes 4194304 | tf_op jit(solution)/shard_map/mul | solution.py:125
  109.3 4.4 %fusion.6 = f32[128,64,64]{2,1,0:T(8,128)} fusion(s32[128,32]{1,0:T(8,128)S(1)} %copy.108, s32[128,32]{1,0:T(8,128)S(1)} %copy.107), kind=kOutput, calls=%fused_computation.10 | convolution fusion | flops 34078720 | bytes 2129920 | tf_op jit(solution)/shard_map/bik,bij->bkj/dot_general | solution.py:132
  113.7 4.8 %copy.109 = f32[128,64,64]{0,2,1:T(8,128)} copy(f32[128,64,64]{2,1,0:T(8,128)} %fusion.6) | data formatting | bytes 4194304 | tf_op jit(solution)/shard_map/bik,bij->bkj/dot_general | solution.py:132
  120.1 2.6 %reshape.324 = f32[64,128,64]{2,1,0:T(8,128)} reshape(f32[64,8,1024]{2,1,0:T(8,128)S(1)} %copy.103) | data formatting | bytes 4194304 | tf_op jit(solution)/shard_map/convert_element_type | solution.py:125
  122.7 6.5 %add.392 = f32[64,128,64]{2,1,0:T(8,128)} add(f32[64,128,64]{2,1,0:T(8,128)} %mul.245, f32[64,128,64]{2,1,0:T(8,128)} %reshape.324) | non-fusion elementwise | flops 524288 | bytes 6291456 | tf_op jit(solution)/shard_map/add | solution.py:125
  129.2 4.2 %copy.105 = f32[64,128,64]{1,0,2:T(8,128)} copy(f32[64,128,64]{2,1,0:T(8,128)} %add.392) | data formatting | bytes 4194304 | tf_op jit(solution)/shard_map/add | solution.py:125
  133.4 2.9 %fusion.56 = f32[128,64,64]{0,2,1:T(8,128)S(1)} fusion(f32[64,128,64]{1,0,2:T(8,128)} %copy.105, f32[64]{0:T(128)S(1)} %add_multiply_fusion, pred[64]{0:T(512)(128)(4,1)S(1)} %iota_compare_fusion.11), kind=kOutput, calls=%fused_computation.150 | convolution fusion | flops 201347072 | bytes 4194624 | tf_op jit(solution)/shard_map/kn,nbm,jm->bkj/dot_general | solution.py:127
  136.3 4.3 %fusion.177 = (f32[128,64,64]{0,2,1:T(8,128)}, f32[128,64,64]{0,2,1:T(8,128)}) fusion(f32[128,64,64]{0,2,1:T(8,128)S(1)} %copy-done.2, f32[64]{0:T(128)S(1)} %add_multiply_fusion, pred[64]{0:T(512)(128)(4,1)S(1)} %iota_compare_fusion.11, f32[128,64,64]{0,2,1:T(8,128)S(1)} %fusion.56), kind=kOutput, calls=%fused_computation.309 | convolution fusion | flops 201871360 | bytes 8388928 | tf_op jit(solution)/shard_map/kn,nbm,jm->bkj/dot_general | solution.py:127
  140.7 5.6 %copy.115 = f32[128,64,64]{2,1,0:T(8,128)} copy(f32[128,64,64]{0,2,1:T(8,128)} %get-tuple-element.53) | data formatting | bytes 4194304 | tf_op jit(solution)/shard_map/kn,nbm,jm->bkj/dot_general | solution.py:127
  146.2 5.0 %select_reduce_fusion = f32[128,32]{1,0:T(8,128)S(1)} fusion(f32[128,64,64]{2,1,0:T(8,128)} %copy.115, s32[128,32]{1,0:T(8,128)S(1)} %copy.108, s32[128,32]{1,0:T(8,128)S(1)} %copy.107), kind=kOutput, calls=%fused_computation.7 | convolution fusion | flops 101707776 | bytes 2146304 | tf_op jit(solution)/shard_map/bik,bkj->bij/dot_general | solution.py:133
  151.4 29.7 %all_to_all.39 = f32[64,1,128]{2,1,0:T(1,128)S(1)} all-to-all(f32[64,1,128]{2,1,0:T(1,128)S(1)} %bitcast.233), channel_id=1, replica_groups=mesh['zh'=2,'x'=4,'zl'=4,'y'=8,'core'=2] {'zl','y','core'}, dimensions={0} | all-to-all | bytes 65536 | tf_op jit(solution)/shard_map/all_to_all | solution.py:17
  184.2 4.6 %all-to-all-start.5 = ((bf16[32,64,128]{2,1,0:T(8,128)(2,1)}), bf16[32,64,128]{2,1,0:T(8,128)(2,1)}, u32[]{:S(2)}, u32[]{:S(2)}) async-start(bf16[32,64,128]{2,1,0:T(8,128)(2,1)} %broadcast_in_dim.74), calls=%async_computation.5 | async-start | bytes 1048576 | tf_op jit(solution)/shard_map/all_to_all | solution.py:17
  188.8 1.6 reshape.323
  190.4 3.8 %fusion.2 = f32[128,64,64]{0,2,1:T(8,128)S(1)} fusion(f32[128,64,64]{0,2,1:T(8,128)} %get-tuple-element.52, f32[64]{0:T(128)S(1)} %add_multiply_fusion, pred[64]{0:T(512)(128)(4,1)S(1)} %iota_compare_fusion.11), kind=kOutput, calls=%fused_computation.2 | convolution fusion | flops 201347072 | bytes 4194624 | tf_op jit(solution)/shard_map/kn,bkj,jm->nbm/dot_general | solution.py:135
  194.2 2.2 %fusion.8 = f32[64,128,64]{1,2,0:T(8,128)S(1)} fusion(f32[128,64,64]{0,2,1:T(8,128)S(1)} %fusion.2, f32[64]{0:T(128)S(1)} %add_multiply_fusion, pred[64]{0:T(512)(128)(4,1)S(1)} %iota_compare_fusion.11), kind=kOutput, calls=%fused_computation.15 | convolution fusion | flops 201347072 | bytes 4194624 | tf_op jit(solution)/shard_map/kn,bkj,jm->nbm/dot_general | solution.py:135
  196.5 2.7 %copy.114 = f32[64,128,64]{2,1,0:T(8,128)} copy(f32[64,128,64]{1,2,0:T(8,128)S(1)} %fusion.8) | data formatting | bytes 4194304 | tf_op jit(solution)/shard_map/kn,bkj,jm->nbm/transpose | solution.py:135
  199.2 3.6 %reshape.316 = f32[1,1,64,8192]{3,2,1,0:T(8,128)S(1)} reshape(f32[64,128,64]{2,1,0:T(8,128)} %copy.114) | data formatting | bytes 4194304 | tf_op jit(solution)/shard_map/reshape | solution.py:136
  202.8 3.4 %all-to-all-done.5 = bf16[32,64,128]{2,1,0:T(8,128)(2,1)} async-done(((bf16[32,64,128]{2,1,0:T(8,128)(2,1)}), bf16[32,64,128]{2,1,0:T(8,128)(2,1)}, u32[]{:S(2)}, u32[]{:S(2)}) %all-to-all-start.5) | async-done | bytes 524320 | tf_op jit(solution)/shard_map/all_to_all | solution.py:17
  206.2 1.9 collective-permute-start.1
  208.1 2.9 %subtract_convert_fusion = bf16[1,1,64,8192]{3,2,1,0:T(8,128)(2,1)} fusion(f32[1,1,64,8192]{3,2,1,0:T(8,128)S(1)} %reshape.316, f32[1,1,64,8192]{3,2,1,0:T(8,128)} %reshape.323, bf16[1,1,64,8192]{3,2,1,0:T(8,128)(2,1)S(1)} %copy-done.5), kind=kLoop, calls=%fused_computation.8 | loop fusion | flops 2621440 | bytes 6291456 | tf_op jit(solution)/shard_map/convert_element_type | solution.py:136
  213.4 1.6 broadcast_in_dim_reshape.8
  (159 shorter events, 27.8 us)
Async XLA Ops:
  0.6 1.2 copy-start
  27.1 3.8 %collective-permute-start = (bf16[8,32,1024]{2,1,0:T(8,128)(2,1)S(1)}, bf16[8,32,1024]{2,1,0:T(8,128)(2,1)S(1)}, u32[]{:S(2)}, u32[]{:S(2)}) collective-permute-start(bf16[8,32,1024]{2,1,0:T(8,128)(2,1)S(1)} %all_to_all.37), channel_id=1, source_target_pairs={{0,1},{1,0},{2,3},{3,2},{4,5},{5,4},{6,7},{7,6},{8,9},{9,8},{10,11... | collective-permute-start | bytes 1572872 | tf_op jit(solution)/shard_map/ppermute | solution.py:21
  31.1 1.1 copy-start.6
  31.1 1.1 copy-start.7
  54.3 19.4 %all-to-all-start.2 = ((bf16[8,64,512]{2,1,0:T(8,128)(2,1)}), bf16[8,64,512]{2,1,0:T(8,128)(2,1)S(1)}, u32[]{:S(2)}, u32[]{:S(2)}) async-start(bf16[8,64,512]{2,1,0:T(8,128)(2,1)} %broadcast_in_dim.67), calls=%async_computation.2 | async-start | bytes 1048576 | tf_op jit(solution)/shard_map/all_to_all | solution.py:17
  91.0 1.6 copy-start.3
  91.1 2.2 %copy-start.4 = (f32[512,1024]{1,0:T(8,128)S(1)}, f32[512,1024]{1,0:T(8,128)}, u32[]{:S(2)}) copy-start(f32[512,1024]{1,0:T(8,128)} %fusion.178) | copy-start | bytes 6291460
  95.1 23.5 %all-to-all-start.3 = ((bf16[8,64,1024]{2,1,0:T(8,128)(2,1)}), bf16[8,64,1024]{2,1,0:T(8,128)(2,1)S(1)}, u32[]{:S(2)}, u32[]{:S(2)}) async-start(bf16[8,64,1024]{2,1,0:T(8,128)(2,1)} %bitcast.170), calls=%async_computation.3 | async-start | bytes 2097152 | tf_op jit(solution)/shard_map/all_to_all | solution.py:17
  106.0 3.0 %copy-start.8 = (s32[1,1,128,32]{2,3,1,0:T(8,128)S(1)}, s32[1,1,128,32]{2,3,1,0:T(8,128)}, u32[]{:S(2)}) copy-start(s32[1,1,128,32]{2,3,1,0:T(8,128)} %param.9) | copy-start | bytes 49156
  133.4 2.9 %copy-start.2 = (f32[128,64,64]{0,2,1:T(8,128)S(1)}, f32[128,64,64]{0,2,1:T(8,128)}, u32[]{:S(2)}) copy-start(f32[128,64,64]{0,2,1:T(8,128)} %copy.109) | copy-start | bytes 6291460
  184.2 22.0 %all-to-all-start.5 = ((bf16[32,64,128]{2,1,0:T(8,128)(2,1)}), bf16[32,64,128]{2,1,0:T(8,128)(2,1)}, u32[]{:S(2)}, u32[]{:S(2)}) async-start(bf16[32,64,128]{2,1,0:T(8,128)(2,1)} %broadcast_in_dim.74), calls=%async_computation.5 | async-start | bytes 1048576 | tf_op jit(solution)/shard_map/all_to_all | solution.py:17
  199.2 8.9 %copy-start.5 = (bf16[1,1,64,8192]{3,2,1,0:T(8,128)(2,1)S(1)}, bf16[1,1,64,8192]{3,2,1,0:T(8,128)(2,1)}, u32[]{:S(2)}) copy-start(bf16[1,1,64,8192]{3,2,1,0:T(8,128)(2,1)} %param.8) | copy-start | bytes 3145732
  206.2 4.8 %collective-permute-start.1 = (bf16[32,64,128]{2,1,0:T(8,128)(2,1)}, bf16[32,64,128]{2,1,0:T(8,128)(2,1)S(1)}, u32[]{:S(2)}, u32[]{:S(2)}) collective-permute-start(bf16[32,64,128]{2,1,0:T(8,128)(2,1)} %all-to-all-done.5), channel_id=1, source_target_pairs={{0,1},{1,0},{2,3},{3,2},{4,5},{5,4},{6,7},{7,6},{8,9},{9,8},{10,11... | collective-permute-start | bytes 1572872 | tf_op jit(solution)/shard_map/ppermute | solution.py:21
  212.2 2.8 %copy-start.1 = (bf16[1,64,8192]{2,1,0:T(8,128)(2,1)S(1)}, bf16[1,64,8192]{2,1,0:T(8,128)(2,1)}, u32[]{:S(2)}) copy-start(bf16[1,64,8192]{2,1,0:T(8,128)(2,1)} %param.7) | copy-start | bytes 3145732

commit v2 on v1

v2 whole, which is shorter than its diff:
```python
import math

import jax
import jax.numpy as jnp
import numpy as np
from jax import lax
from jax.experimental import pallas as pl
from jax.experimental.pallas import tpu as pltpu
from jax.sharding import Mesh, PartitionSpec as P

DECAY = 0.999
S = ("zh", "x")
CHIP = ("zl", "y")
DP = ("zl", "y", "core")
F32 = jnp.float32
BF = jnp.bfloat16
LAYERS = 8


def a2a(value, axis):
    return lax.all_to_all(value, axis, 0, 0, tiled=True)


def swap_cores(value):
    return lax.ppermute(value, "core", [(0, 1), (1, 0)])


def mm(a, b):
    return lax.dot_general(a, b, (((1,), (0,)), ((), ())), preferred_element_type=F32)


def mm_nt(a, b):
    return lax.dot_general(a, b, (((1,), (1,)), ((), ())), preferred_element_type=F32)


def split(value):
    high = value.astype(BF)
    return high, (value - high.astype(F32)).astype(BF)


def dct_tables():
    n = np.arange(64)
    basis = np.cos(np.pi * (n[None, :] + 0.5) * n[:, None] / 64) * math.sqrt(2.0 / 64)
    basis[0] *= math.sqrt(0.5)
    return basis.astype(np.float32)


def pair(value):
    high = value.astype(jnp.bfloat16)
    low = (value - high.astype(np.float32)).astype(jnp.bfloat16)
    return high, low


def row_table(basis):
    high, low = pair(basis)
    return np.concatenate([high, high, low], axis=1)


def col_table(basis, count):
    high, low = pair(np.kron(np.eye(count, dtype=np.float32), basis))
    return np.concatenate([high, high, low], axis=0)


def by_rows(table, value):
    high, low = split(value)
    return mm(table, jnp.concatenate([high, low, high], axis=0))


def by_cols(value, table):
    high, low = split(value)
    return mm(jnp.concatenate([high, low, high], axis=1), table)


def whole(count):
    return [pl.BlockSpec(memory_space=pltpu.VMEM)] * count


SCALAR = pl.BlockSpec(memory_space=pltpu.SMEM)


def relay_kernel(core, got, x, g, mine, other, out, rhs):
    rows = 64
    at_mine = pl.multiple_of(core[0] * 32, 32)
    at_other = pl.multiple_of(32 - core[0] * 32, 32)
    for l in range(LAYERS):
        rhs[pl.ds(l * rows + at_mine, 32)] = mine[l]
        rhs[pl.ds(l * rows + at_other, 32)] = other[l]
    rhs[512:640] = g[...]
    rhs[640:768] = x[...]
    zero = jnp.zeros((rows, 128), BF)

    def block(l, p):
        if p < 2:
            return got[l, :, 256 + 128 * p : 384 + 128 * p]
        if l == 7:
            return got[0, :, 128 * p : 128 * p + 128]
        return got[7 - l, :, 384:512]

    acts, hs = [zero] * LAYERS, []
    for l in range(LAYERS):
        h = got[l, :, 0:128].astype(F32)
        pairs = range((l + 1) // 2)
        if len(pairs):
            left = jnp.concatenate([block(l, p) for p in pairs], axis=1)
            right = jnp.concatenate(acts[: 2 * len(pairs)], axis=0)
            h = h + mm(left, right)
        hs.append(h)
        acts[l] = (h * (1.0 / (1.0 + jnp.exp(-h)))).astype(BF)

    turned = {}
    for p in range(4):
        for q in range(p, 4):
            upper = zero if p == q else block(2 * q, p)
            both = jnp.concatenate([upper, block(2 * q + 1, p)], axis=0)
            turned[p, q] = both.T
    deltas = [zero] * LAYERS
    for l in reversed(range(LAYERS)):
        e = got[l, :, 128:256].astype(F32)
        pairs = range((l + 1) // 2, 4)
        if len(pairs):
            lo = rows * (l % 2)
            left = jnp.concatenate([turned[l // 2, q][lo : lo + rows] for q in pairs], axis=1)
            right = jnp.concatenate(deltas[2 * pairs[0] :], axis=0)
            e = e + mm(left, right)
        s = 1.0 / (1.0 + jnp.exp(-hs[l]))
        deltas[l] = (e * (s * (1.0 + hs[l] * (1.0 - s)))).astype(BF)

    act = jnp.concatenate(acts, axis=0)
    delta = jnp.concatenate(deltas, axis=0)
    row_layer = lax.broadcasted_iota(jnp.int32, (512, 512), 0) // rows
    col_layer = lax.broadcasted_iota(jnp.int32, (512, 512), 1) // rows
    cross = jnp.where(
        row_layer < col_layer, mm_nt(act, delta), jnp.where(row_layer > col_layer, mm_nt(delta, act), 0.0)
    ).astype(BF)
    lhs = jnp.concatenate([cross, act, delta], axis=1)
    for n in range(4):
        cols = slice(256 * n, 256 * n + 256)
        grads = mm(lhs, rhs[:, cols]).astype(BF)
        for l in range(LAYERS):
            out[l, :, cols] = grads[rows * l : rows * l + rows]


def coef_kernel(grad, momentum, keep, row_t, col_t, coef, sent):
    lane = lax.broadcasted_iota(jnp.int32, (1, 128), 1)
    sub = lax.broadcasted_iota(jnp.int32, (8, 128), 0)
    for s in range(8):
        fresh = DECAY * momentum[:, 1024 * s : 1024 * s + 1024].astype(F32) + grad[s].astype(F32)
        y = by_cols(jnp.concatenate([fresh[:, 256 * q : 256 * q + 256] for q in range(4)], axis=0), col_t[...])
        for q in range(4):
            z = by_rows(row_t[...], y[64 * q : 64 * q + 64])
            at = 1024 * s + 256 * q
            coef[:, at : at + 256] = z
            for u in range(2):
                t = 8 * s + 2 * q + u
                where = keep[t : t + 1, :]
                row = jnp.broadcast_to(where // 64, (8, 128))
                col = jnp.broadcast_to(where % 64 + (lane // 32) % 2 * 64, (8, 128))
                total = jnp.zeros((8, 128), F32)
                for r in range(8):
                    tile = z[8 * r : 8 * r + 8, 128 * u : 128 * u + 128]
                    picked = jnp.take_along_axis(tile, col, axis=1, mode="promise_in_bounds")
                    total = total + jnp.where(sub + 8 * r == row, picked, 0.0)
                value = jnp.sum(total, axis=0, keepdims=True)
                sent[t : t + 1, :] = jnp.where(lane < 64, value, where.astype(F32))


def rest_kernel(coef, keep, row_t, col_t, out):
    lane = lax.broadcasted_iota(jnp.int32, (1, 128), 1)
    row_id = lax.broadcasted_iota(jnp.int32, (64, 128), 0)
    col_id = lax.broadcasted_iota(jnp.int32, (128, 128), 0)
    for s in range(8):
        parts = []
        for q in range(4):
            halves = []
            for u in range(2):
                t = 8 * s + 2 * q + u
                where = keep[t : t + 1, :]
                row_hot = jnp.where((row_id == where // 64) & (lane < 64), 1.0, 0.0).astype(BF)
                col_hot = jnp.where(col_id == where % 64 + (lane // 32) % 2 * 64, 1.0, 0.0).astype(BF)
                kept = mm_nt(row_hot, col_hot)
                halves.append(jnp.where(kept > 0.5, 0.0, coef[:, 128 * t : 128 * t + 128]))
            parts.append(by_rows(row_t[...], jnp.concatenate(halves, axis=1)))
        y = by_cols(jnp.concatenate(parts, axis=0), col_t[...]).astype(BF)
        for q in range(4):
            at = 1024 * s + 256 * q
            out[:, at : at + 256] = y[64 * q : 64 * q + 64]


def owner_kernel(seen, row_t, col_t, out):
    lane = lax.broadcasted_iota(jnp.int32, (32, 128), 1)
    top, bottom = seen[0:32, :], seen[32:64, :]
    value = jnp.where(lane < 64, top, pltpu.roll(bottom, 64, 1))
    where = jnp.where(lane < 64, pltpu.roll(top, 64, 1), bottom).astype(jnp.int32)
    row = where // 64
    col = where % 64 + (lane // 32) % 2 * 64
    row_id = lax.broadcasted_iota(jnp.int32, (64, 128), 0)
    col_id = lax.broadcasted_iota(jnp.int32, (128, 128), 0)
    total = jnp.zeros((128, 128), F32)
    for t in range(0, 32, 2):
        lefts, rights = [], []
        for v in (t, t + 1):
            spread = jnp.where(row_id == row[v : v + 1, :], value[v : v + 1, :], 0.0)
            lefts.append(jnp.concatenate(split(spread), axis=0))
            rights.append(jnp.where(col_id == col[v : v + 1, :], 1.0, 0.0).astype(BF))
        total = total + mm_nt(jnp.concatenate(lefts, axis=1), jnp.concatenate(rights, axis=1))
    summed = total[0:64] + total[64:128]
    decoded = by_cols(by_rows(row_t[...], summed), col_t[...]).astype(BF)
    for m in range(out.shape[0]):
        out[m] = decoded


def join_kernel(core, here, there, out):
    def place(first, second):
        for m in range(32):
            out[:, 256 * m : 256 * m + 128] = first[m]
            out[:, 256 * m + 128 : 256 * m + 256] = second[m]

    @pl.when(core[0] == 0)
    def _():
        place(here, there)

    @pl.when(core[0] == 1)
    def _():
        place(there, here)


def call(kernel, name, out_shape, in_specs, args, scratch=(), flops=0):
    outs = jax.tree.map(lambda _: pl.BlockSpec(memory_space=pltpu.VMEM), out_shape)
    return pl.pallas_call(
        kernel,
        out_shape=out_shape,
        in_specs=in_specs,
        out_specs=outs,
        scratch_shapes=list(scratch),
        name=name,
        compiler_params=pltpu.CompilerParams(vmem_limit_bytes=32 * 1024 * 1024),
        cost_estimate=pl.CostEstimate(flops=flops, bytes_accessed=0, transcendentals=0),
    )(*args)


def local(inputs, cotangent, weights, momentum, keep_index):
    core = lax.axis_index("core").astype(jnp.int32)
    core_at = core.reshape(1)
    weight = weights[0]
    rows, width = weight.shape
    cols = width // LAYERS
    full = LAYERS * rows
    struct = jax.ShapeDtypeStruct

    half = lax.dynamic_slice_in_dim(weight, core * (rows // 2), rows // 2, 0)
    mine = a2a(half.reshape(rows // 2, LAYERS, cols).transpose(1, 0, 2), S)
    other = swap_cores(mine)
    w = jnp.concatenate(
        [jnp.where(core == 0, mine, other), jnp.where(core == 0, other, mine)], axis=1
    ).reshape(full, cols)

    proj = mm_nt(w, jnp.concatenate([inputs, cotangent], axis=0)).astype(BF).reshape(LAYERS, rows, 256)
    gram = mm_nt(w, w).astype(BF).reshape(LAYERS, rows, full)
    packed = jnp.stack(
        [gram[7, :, 256:]]
        + [jnp.concatenate([gram[l, :, :128], gram[7 - l, :, 256:384]], axis=1) for l in (1, 2)]
        + [gram[l, :, :256] for l in range(3, LAYERS)]
    )
    payload = jnp.concatenate([proj, packed], axis=2)
    got = jnp.sum(a2a(payload, S).astype(F32), axis=0).astype(BF)
    got = a2a(jnp.broadcast_to(got[None], (LAYERS,) + got.shape), S)

    grads = call(
        relay_kernel,
        "relay",
        struct((LAYERS, rows, cols), BF),
        [SCALAR] + whole(5),
        (core_at, got, inputs, cotangent, mine, other),
        [pltpu.VMEM((768, cols), BF)],
        2 * 512 * 768 * 1024,
    )
    grad = a2a(grads, S)

    basis = dct_tables()
    keep = keep_index[0, 0].reshape(64, 64)
    keep = jnp.concatenate([keep, keep], axis=1)
    coef, sent = call(
        coef_kernel,
        "coef",
        (struct((rows, width), F32), struct((64, 128), F32)),
        whole(5),
        (grad, momentum[0, 0], keep, row_table(basis), col_table(basis.T, 4)),
        (),
        2 * 2048 * 768 * 256,
    )
    seen = a2a(sent, DP)
    momentum_out = call(
        rest_kernel,
        "rest",
        struct((rows, width), BF),
        whole(4),
        (coef, keep, row_table(basis.T), col_table(basis, 4)),
        (),
        2 * 2048 * 768 * 256 * 4,
    )

    spread = call(
        owner_kernel,
        "owner",
        struct((32, 64, 128), BF),
        whole(3),
        (seen, row_table(basis.T), col_table(basis, 2)),
        (),
        2 * 64 * 128 * 4096,
    )
    here = a2a(spread, CHIP)
    there = swap_cores(here)
    update = call(
        join_kernel, "join", struct((rows, width), BF), [SCALAR] + whole(2), (core_at, here, there), (), 1000
    )
    return (momentum_out[None, None], update[None, None])


def solution(mesh):
    fine = Mesh(mesh.devices.reshape(2, 4, 4, 8, 2), ("zh", "x", "zl", "y", "core"))
    return jax.shard_map(
        local,
        mesh=fine,
        in_specs=(
            P(DP, S),
            P(DP, S),
            P(S, None, None),
            P(S, DP, None, None),
            P(S, DP, None, None),
        ),
        out_specs=(P(S, DP, None, None), P(S, DP, None, None)),
        check_vma=False,
    )
```

time: 217 us -> 168 us (0.77)
  matrix products: 43 us -> 1.22 us
  blocking collectives: 74.9 us -> 115 us
  local copies, waits for them, and re-layouts: 40.2 us -> 3.32 us
  Pallas kernels: 0 us -> 17.1 us
  starting transfers between devices: 27.3 us -> 13.5 us
  other arithmetic: 13 us -> 0.35 us
    dot_general x73 -> x2, matrix products: 43 us -> 1.22 us  [mm_nt(): lax.dot_general(a, b, (((1,), (1,)), ((), ())), preferred_element_type=F32)]
    all_to_all x3 -> x5, blocking collectives: 74.9 us -> 115 us  [a2a(): return lax.all_to_all(value, axis, 0, 0, tiled=True)]
    pallas_call x0 -> x5, Pallas kernels: none -> 17.1 us  [call(): pl.pallas_call(kernel, out_shape=out_shape, in_specs=in_specs, out_specs=...]
    all_to_all x3 -> x1, starting transfers between devices: 23.5 us -> 9.53 us  [a2a(): return lax.all_to_all(value, axis, 0, 0, tiled=True)]
    dot_general x3 -> x0, local copies, waits for them, and re-layouts: 10.7 us -> none  [the longest x1 5.57 us: local(): jnp.einsum('kn,nbm,jm->bkj', table, blocks, table, precision=lax.Precisio...]
    add x1 -> x0, other arithmetic: 6.51 us -> none  [local(): fresh = DECAY * momentum[0, 0].astype(F32) + grad.astype(F32)]
    convert_element_type x7 -> x0, local copies, waits for them, and re-layouts: 5.73 us -> none  [the longest x3 5.43 us: local(): fresh = DECAY * momentum[0, 0].astype(F32) + grad.astype(F32)]
    transpose x5 -> x0, local copies, waits for them, and re-layouts: 4.26 us -> none  [the longest x1 2.73 us: local(): jnp.einsum('kn,bkj,jm->nbm', table, coef * mask, table, precision=lax.Pre...]
  transfers between devices with their start and end apart: 5 -> 3, of which waited for: 3 -> 2; matrix products, arithmetic and copies ran while one was open for 14% -> 0% of each run, Pallas kernels for 0% -> 5%
where the time goes in v2:
time: 168 us; the launch traced here: 166 us
  blocking collectives  115 us (68%)
  Pallas kernels  17.1 us (10%)
  waiting for transfers between devices  14.5 us (9%)
  starting transfers between devices  13.5 us (8%)
  local copies, waits for them, and re-layouts  3.32 us (2%)
    all_to_all x5, blocking collectives, a2a(): return lax.all_to_all(value, axis, 0, 0, tiled=True)  115 us
    pallas_call x5, Pallas kernels, call(): pl.pallas_call(kernel, out_shape=out_shape, in_specs=in_specs, out_specs=...  17.1 us
    all_to_all x1, waiting for transfers between devices, a2a(): return lax.all_to_all(value, axis, 0, 0, tiled=True)  12.6 us
    all_to_all x1, starting transfers between devices, a2a(): return lax.all_to_all(value, axis, 0, 0, tiled=True)  9.53 us
    ppermute x2, starting transfers between devices, swap_cores(): return lax.ppermute(value, 'core', [(0, 1), (1, 0)])  4 us
  transfers between devices with their start and end apart: 3, of which 2 were waited for; matrix products, arithmetic and copies ran while one was open for 0% of the time, Pallas kernels for 5%

profile of v2, /device:TPU:6, one launch (start us, length us, event | category | flops | bytes accessed | tf_op | source)
XLA Modules:
  0.0 165.8 jit_solution(3076684457665348418)
XLA Ops:
  0.6 0.0 copy-start
  0.6 1.2 copy-done
  1.9 0.3 copy.19
  2.2 0.3 copy.21
  2.5 24.6 %all_to_all.36.mine = bf16[8,32,1024]{2,1,0:T(8,128)(2,1)S(1)} all-to-all(bf16[8,32,1024]{2,1,0:T(8,128)(2,1)S(1)} %bitcast.39), channel_id=1, replica_groups=mesh['zh'=2,'x'=4,'zl'=4,'y'=8,'core'=2] {'zh','x'}, dimensions={0} | all-to-all | bytes 1048576 | tf_op jit(solution)/shard_map/all_to_all | solution.py:21
  27.1 1.9 %collective-permute-start = (bf16[8,32,1024]{2,1,0:T(8,128)(2,1)S(1)}, bf16[8,32,1024]{2,1,0:T(8,128)(2,1)S(1)}, u32[]{:S(2)}, u32[]{:S(2)}) collective-permute-start(bf16[8,32,1024]{2,1,0:T(8,128)(2,1)S(1)} %all_to_all.36.mine), channel_id=1, source_target_pairs={{0,1},{1,0},{2,3},{3,2},{4,5},{5,4},{6,7},{7,6},{8,9},{9,8},{10,11... | collective-permute-start | bytes 1572872 | tf_op jit(solution)/shard_map/ppermute | solution.py:25
  29.1 1.9 %collective-permute-done.other = bf16[8,32,1024]{2,1,0:T(8,128)(2,1)S(1)} collective-permute-done((bf16[8,32,1024]{2,1,0:T(8,128)(2,1)S(1)}, bf16[8,32,1024]{2,1,0:T(8,128)(2,1)S(1)}, u32[]{:S(2)}, u32[]{:S(2)}) %collective-permute-start) | collective-permute-done | bytes 524320 | tf_op jit(solution)/shard_map/ppermute | solution.py:25
  30.9 0.1 broadcast_select_fusion.1
  31.0 0.1 pad_maximum_fusion
  31.1 0.0 copy-start.1
  31.1 0.0 copy-start.2
  31.1 0.7 convolution_convert_fusion
  31.9 0.1 copy-done.1
  32.0 0.1 copy-done.2
  32.1 0.5 convolution_convert_fusion.1
  32.7 20.5 %all_to_all.37 = bf16[8,64,512]{2,1,0:T(8,128)(2,1)S(1)} all-to-all(bf16[8,64,512]{2,1,0:T(8,128)(2,1)S(1)} %maximum_maximum_fusion), channel_id=1, replica_groups=mesh['zh'=2,'x'=4,'zl'=4,'y'=8,'core'=2] {'zh','x'}, dimensions={0} | all-to-all | bytes 1048576 | tf_op jit(solution)/shard_map/all_to_all | solution.py:21
  53.2 0.1 reduce_sum.12
  53.3 18.5 %all_to_all.38.got = bf16[8,64,512]{2,1,0:T(8,128)(2,1)S(1)} all-to-all(bf16[8,64,512]{2,1,0:T(8,128)(2,1)S(1)} %broadcast_in_dim.12), channel_id=1, replica_groups=mesh['zh'=2,'x'=4,'zl'=4,'y'=8,'core'=2] {'zh','x'}, dimensions={0} | all-to-all | bytes 1048576 | tf_op jit(solution)/shard_map/all_to_all | solution.py:21
  71.8 4.2 %relay.1 = bf16[8,64,1024]{2,1,0:T(8,128)(2,1)} custom-call(s32[1]{0:T(128)} %bitcast.core, bf16[8,64,512]{2,1,0:T(8,128)(2,1)S(1)} %all_to_all.38.got, bf16[128,1024]{1,0:T(8,128)(2,1)S(1)} %copy-done.2, bf16[128,1024]{1,0:T(8,128)(2,1)S(1)} %copy-done.1, bf16[8,32,1024]{2,1,0:T(8,128)(2,1)S(1)} %all_to_all.36.mine, ...), custom_call_target="tpu_custom_call" | custom-call | flops 805306368 | tf_op jit(solution)/shard_map/relay/pallas_call | solution.py:229
  76.0 9.5 %all-to-all-start.3 = ((bf16[8,64,1024]{2,1,0:T(8,128)(2,1)}), bf16[8,64,1024]{2,1,0:T(8,128)(2,1)S(1)}, u32[]{:S(2)}, u32[]{:S(2)}) async-start(bf16[8,64,1024]{2,1,0:T(8,128)(2,1)} %relay.1), calls=%async_computation.3 | async-start | bytes 2097152 | tf_op jit(solution)/shard_map/all_to_all | solution.py:21
  85.6 0.1 copy.17
  85.7 0.1 reshape_squeeze.3
  85.8 0.1 pad_add_fusion.keep
  85.8 12.6 %all-to-all-done.3.grad = bf16[8,64,1024]{2,1,0:T(8,128)(2,1)S(1)} async-done(((bf16[8,64,1024]{2,1,0:T(8,128)(2,1)}), bf16[8,64,1024]{2,1,0:T(8,128)(2,1)S(1)}, u32[]{:S(2)}, u32[]{:S(2)}) %all-to-all-start.3) | async-done | bytes 1048608 | tf_op jit(solution)/shard_map/all_to_all | solution.py:21
  98.4 1.0 copy-done.7
  99.4 2.9 %coef.1 = (f32[64,8192]{1,0:T(8,128)S(1)}, f32[64,128]{1,0:T(8,128)S(1)}) custom-call(bf16[8,64,1024]{2,1,0:T(8,128)(2,1)S(1)} %all-to-all-done.3.grad, bf16[64,8192]{1,0:T(8,128)(2,1)S(1)} %bitcast.36, s32[64,128]{1,0:T(8,128)S(1)} %pad_add_fusion.keep, bf16[64,192]{1,0:T(8,128)(2,1)S(1)} %copy-done.8, bf16[768,256]{1,0:T(8,128)(2,1)S(1)} %copy-done.7), custom_call_target="tpu_custom_call" | custom-call | flops 805306368 | tf_op jit(solution)/shard_map/coef/pallas_call | solution.py:229
  102.3 30.9 %all_to_all.39 = f32[64,1,128]{2,1,0:T(1,128)S(1)} all-to-all(f32[64,1,128]{2,1,0:T(1,128)S(1)} %bitcast.35), channel_id=1, replica_groups=mesh['zh'=2,'x'=4,'zl'=4,'y'=8,'core'=2] {'zl','y','core'}, dimensions={0} | all-to-all | bytes 65536 | tf_op jit(solution)/shard_map/all_to_all | solution.py:21
  133.3 1.0 owner.1
  134.3 20.4 %all_to_all.40.here = bf16[32,64,128]{2,1,0:T(8,128)(2,1)S(1)} all-to-all(bf16[32,64,128]{2,1,0:T(8,128)(2,1)S(1)} %owner.1), channel_id=1, replica_groups=mesh['zh'=2,'x'=4,'zl'=4,'y'=8,'core'=2] {'zl','y'}, dimensions={0} | all-to-all | bytes 1048576 | tf_op jit(solution)/shard_map/all_to_all | solution.py:21
  154.7 2.1 %collective-permute-start.1 = (bf16[32,64,128]{2,1,0:T(8,128)(2,1)S(1)}, bf16[32,64,128]{2,1,0:T(8,128)(2,1)S(1)}, u32[]{:S(2)}, u32[]{:S(2)}) collective-permute-start(bf16[32,64,128]{2,1,0:T(8,128)(2,1)S(1)} %all_to_all.40.here), channel_id=1, source_target_pairs={{0,1},{1,0},{2,3},{3,2},{4,5},{5,4},{6,7},{7,6},{8,9},{9,8},{10,11... | collective-permute-start | bytes 1572872 | tf_op jit(solution)/shard_map/ppermute | solution.py:25
  156.8 7.8 %rest.1 = bf16[64,8192]{1,0:T(8,128)(2,1)} custom-call(f32[64,8192]{1,0:T(8,128)S(1)} %get-tuple-element.4.coef, s32[64,128]{1,0:T(8,128)S(1)} %pad_add_fusion.keep, bf16[64,192]{1,0:T(8,128)(2,1)S(1)} %copy-done.4, bf16[768,256]{1,0:T(8,128)(2,1)S(1)} %copy-done.6), custom_call_target="tpu_custom_call" | custom-call | flops 3221225472 | tf_op jit(solution)/shard_map/rest/pallas_call | solution.py:229
  164.6 1.2 join.1
  (21 shorter events, 0.2 us)
Async XLA Ops:
  0.6 1.2 copy-start
  27.1 3.8 %collective-permute-start = (bf16[8,32,1024]{2,1,0:T(8,128)(2,1)S(1)}, bf16[8,32,1024]{2,1,0:T(8,128)(2,1)S(1)}, u32[]{:S(2)}, u32[]{:S(2)}) collective-permute-start(bf16[8,32,1024]{2,1,0:T(8,128)(2,1)S(1)} %all_to_all.36.mine), channel_id=1, source_target_pairs={{0,1},{1,0},{2,3},{3,2},{4,5},{5,4},{6,7},{7,6},{8,9},{9,8},{10,11... | collective-permute-start | bytes 1572872 | tf_op jit(solution)/shard_map/ppermute | solution.py:25
  31.1 1.0 copy-start.1
  31.1 1.0 copy-start.2
  71.8 13.8 %copy-start.9 = (s32[1,1,128,32]{2,3,1,0:T(8,128)S(1)}, s32[1,1,128,32]{2,3,1,0:T(8,128)}, u32[]{:S(2)}) copy-start(s32[1,1,128,32]{2,3,1,0:T(8,128)} %param.15) | copy-start | bytes 49156
  71.8 26.6 %copy-start.8 = (bf16[64,192]{1,0:T(8,128)(2,1)S(1)}, bf16[64,192]{1,0:T(8,128)(2,1)}, u32[]{:S(2)}) copy-start(bf16[64,192]{1,0:T(8,128)(2,1)} %constant.24.clone.row_t) | copy-start | bytes 73732
  76.0 22.4 %copy-start.5 = (bf16[1,1,64,8192]{3,2,1,0:T(8,128)(2,1)S(1)}, bf16[1,1,64,8192]{3,2,1,0:T(8,128)(2,1)}, u32[]{:S(2)}) copy-start(bf16[1,1,64,8192]{3,2,1,0:T(8,128)(2,1)} %param.14) | copy-start | bytes 3145732
  76.0 22.4 %all-to-all-start.3 = ((bf16[8,64,1024]{2,1,0:T(8,128)(2,1)}), bf16[8,64,1024]{2,1,0:T(8,128)(2,1)S(1)}, u32[]{:S(2)}, u32[]{:S(2)}) async-start(bf16[8,64,1024]{2,1,0:T(8,128)(2,1)} %relay.1), calls=%async_computation.3 | async-start | bytes 2097152 | tf_op jit(solution)/shard_map/all_to_all | solution.py:21
  85.6 47.7 %copy-start.3 = (bf16[384,128]{1,0:T(8,128)(2,1)S(1)}, bf16[384,128]{1,0:T(8,128)(2,1)}, u32[]{:S(2)}) copy-start(bf16[384,128]{1,0:T(8,128)(2,1)} %constant.28.clone.col_t) | copy-start | bytes 294916
  85.6 47.7 %copy-start.4 = (bf16[64,192]{1,0:T(8,128)(2,1)S(1)}, bf16[64,192]{1,0:T(8,128)(2,1)}, u32[]{:S(2)}) copy-start(bf16[64,192]{1,0:T(8,128)(2,1)} %constant.26.clone.row_t) | copy-start | bytes 73732
  98.4 1.0 copy-start.7
  99.4 57.4 %copy-start.6 = (bf16[768,256]{1,0:T(8,128)(2,1)S(1)}, bf16[768,256]{1,0:T(8,128)(2,1)}, u32[]{:S(2)}) copy-start(bf16[768,256]{1,0:T(8,128)(2,1)} %constant.27.clone.col_t) | copy-start | bytes 1179652
  154.7 9.9 %collective-permute-start.1 = (bf16[32,64,128]{2,1,0:T(8,128)(2,1)S(1)}, bf16[32,64,128]{2,1,0:T(8,128)(2,1)S(1)}, u32[]{:S(2)}, u32[]{:S(2)}) collective-permute-start(bf16[32,64,128]{2,1,0:T(8,128)(2,1)S(1)} %all_to_all.40.here), channel_id=1, source_target_pairs={{0,1},{1,0},{2,3},{3,2},{4,5},{5,4},{6,7},{7,6},{8,9},{9,8},{10,11... | collective-permute-start | bytes 1572872 | tf_op jit(solution)/shard_map/ppermute | solution.py:25

commit v3 on v2

--- a/solution.py
+++ b/solution.py
@@ -7,6 +7,7 @@
 from jax.experimental import pallas as pl
 from jax.experimental.pallas import tpu as pltpu
 from jax.sharding import Mesh, PartitionSpec as P
+
 
 DECAY = 0.999
 S = ("zh", "x")
@@ -91,14 +92,14 @@
 
     def block(l, p):
         if p < 2:
-            return got[l, :, 256 + 128 * p : 384 + 128 * p]
+            return got[l % 4, l // 4, :, 256 + 128 * p : 384 + 128 * p]
         if l == 7:
-            return got[0, :, 128 * p : 128 * p + 128]
-        return got[7 - l, :, 384:512]
+            return got[0, 0, :, 128 * p : 128 * p + 128]
+        return got[7 - l, 0, :, 384:512]
 
     acts, hs = [zero] * LAYERS, []
     for l in range(LAYERS):
-        h = got[l, :, 0:128].astype(F32)
+        h = got[l % 4, l // 4, :, 0:128].astype(F32)
         pairs = range((l + 1) // 2)
         if len(pairs):
             left = jnp.concatenate([block(l, p) for p in pairs], axis=1)
@@ -115,7 +116,7 @@
             turned[p, q] = both.T
     deltas = [zero] * LAYERS
     for l in reversed(range(LAYERS)):
-        e = got[l, :, 128:256].astype(F32)
+        e = got[l % 4, l // 4, :, 128:256].astype(F32)
         pairs = range((l + 1) // 2, 4)
         if len(pairs):
             lo = rows * (l % 2)
@@ -140,50 +141,80 @@
             out[l, :, cols] = grads[rows * l : rows * l + rows]
 
 
-def coef_kernel(grad, momentum, keep, row_t, col_t, coef, sent):
+def pick(z, row, col, lane):
+    sub = lax.broadcasted_iota(jnp.int32, (8, 128), 0)
+    row = jnp.broadcast_to(row, (8, 128))
+    col = jnp.broadcast_to(col + (lane // 32) % 2 * 64, (8, 128))
+    first = jnp.broadcast_to(lane < 64, (8, 128))
+    total = jnp.zeros((8, 128), F32)
+    for r in range(8):
+        left, right = (
+            jnp.take_along_axis(
+                z[8 * r : 8 * r + 8, 128 * u : 128 * u + 128], col, axis=1, mode="promise_in_bounds"
+            )
+            for u in range(2)
+        )
+        total = total + jnp.where(sub + 8 * r == row, jnp.where(first, left, right), 0.0)
+    return jnp.sum(total, axis=0, keepdims=True)
+
+
+def choose(field, keep, row_t, col_t, vals):
     lane = lax.broadcasted_iota(jnp.int32, (1, 128), 1)
-    sub = lax.broadcasted_iota(jnp.int32, (8, 128), 0)
     for s in range(8):
-        fresh = DECAY * momentum[:, 1024 * s : 1024 * s + 1024].astype(F32) + grad[s].astype(F32)
-        y = by_cols(jnp.concatenate([fresh[:, 256 * q : 256 * q + 256] for q in range(4)], axis=0), col_t[...])
+        piece = field(s)
+        y = by_cols(jnp.concatenate([piece[:, 256 * q : 256 * q + 256] for q in range(4)], axis=0), col_t[...])
         for q in range(4):
+            t = 4 * s + q
             z = by_rows(row_t[...], y[64 * q : 64 * q + 64])
-            at = 1024 * s + 256 * q
-            coef[:, at : at + 256] = z
-            for u in range(2):
-                t = 8 * s + 2 * q + u
-                where = keep[t : t + 1, :]
-                row = jnp.broadcast_to(where // 64, (8, 128))
-                col = jnp.broadcast_to(where % 64 + (lane // 32) % 2 * 64, (8, 128))
-                total = jnp.zeros((8, 128), F32)
-                for r in range(8):
-                    tile = z[8 * r : 8 * r + 8, 128 * u : 128 * u + 128]
-                    picked = jnp.take_along_axis(tile, col, axis=1, mode="promise_in_bounds")
-                    total = total + jnp.where(sub + 8 * r == row, picked, 0.0)
-                value = jnp.sum(total, axis=0, keepdims=True)
-                sent[t : t + 1, :] = jnp.where(lane < 64, value, where.astype(F32))
-
-
-def rest_kernel(coef, keep, row_t, col_t, out):
+            where = keep[t : t + 1, :]
+            vals[t : t + 1, :] = pick(z, where // 64, where % 64, lane)
+
+
+def past_kernel(momentum, keep, row_t, col_t, vals):
+    choose(lambda s: DECAY * momentum[:, 1024 * s : 1024 * s + 1024].astype(F32), keep, row_t, col_t, vals)
+
+
+def coef_kernel(grad, past, keep, row_t, col_t, vals, sent):
+    choose(lambda s: grad[s].astype(F32), keep, row_t, col_t, vals)
+    value = vals[...] + past[...]
+    vals[...] = value
+    where = keep[...].astype(F32)
+    first = lax.broadcasted_iota(jnp.int32, (32, 128), 1) < 64
+    sent[0:32, :] = jnp.where(first, value, pltpu.roll(where, 64, 1))
+    sent[32:64, :] = jnp.where(first, pltpu.roll(value, 64, 1), where)
+
+
+def half_kernel(core, weight, out, sems):
+    at = pl.multiple_of(core[0] * 32, 32)
+    copies = [
+        pltpu.make_async_copy(weight.at[pl.ds(at, 32), pl.ds(1024 * s, 1024)], out.at[s], sems.at[s])
+        for s in range(LAYERS)
+    ]
+    for copy in copies:
+        copy.start()
+    for copy in copies:
+        copy.wait()
+
+
+def rest_kernel(vals, keep, momentum, grad, row_t, col_t, out):
     lane = lax.broadcasted_iota(jnp.int32, (1, 128), 1)
     row_id = lax.broadcasted_iota(jnp.int32, (64, 128), 0)
-    col_id = lax.broadcasted_iota(jnp.int32, (128, 128), 0)
+    col_id = lax.broadcasted_iota(jnp.int32, (256, 128), 0)
     for s in range(8):
         parts = []
         for q in range(4):
-            halves = []
-            for u in range(2):
-                t = 8 * s + 2 * q + u
-                where = keep[t : t + 1, :]
-                row_hot = jnp.where((row_id == where // 64) & (lane < 64), 1.0, 0.0).astype(BF)
-                col_hot = jnp.where(col_id == where % 64 + (lane // 32) % 2 * 64, 1.0, 0.0).astype(BF)
-                kept = mm_nt(row_hot, col_hot)
-                halves.append(jnp.where(kept > 0.5, 0.0, coef[:, 128 * t : 128 * t + 128]))
-            parts.append(by_rows(row_t[...], jnp.concatenate(halves, axis=1)))
-        y = by_cols(jnp.concatenate(parts, axis=0), col_t[...]).astype(BF)
+            t = 4 * s + q
+            where = keep[t : t + 1, :]
+            spread = jnp.where(row_id == where // 64, vals[t : t + 1, :], 0.0)
+            col_hot = jnp.where(col_id == where % 64 + lane // 32 * 64, 1.0, 0.0).astype(BF)
+            both = mm_nt(jnp.concatenate(split(spread), axis=0), col_hot)
+            parts.append(by_rows(row_t[...], both[0:64] + both[64:128]))
+        y = by_cols(jnp.concatenate(parts, axis=0), col_t[...])
         for q in range(4):
-            at = 1024 * s + 256 * q
-            out[:, at : at + 256] = y[64 * q : 64 * q + 64]
+            at = 256 * q
+            cols = slice(1024 * s + at, 1024 * s + at + 256)
+            fresh = DECAY * momentum[:, cols].astype(F32) + grad[s, :, at : at + 256].astype(F32)
+            out[:, cols] = (fresh - y[64 * q : 64 * q + 64]).astype(BF)
 
 
 def owner_kernel(seen, row_t, col_t, out):
@@ -212,8 +243,9 @@
 def join_kernel(core, here, there, out):
     def place(first, second):
         for m in range(32):
-            out[:, 256 * m : 256 * m + 128] = first[m]
-            out[:, 256 * m + 128 : 256 * m + 256] = second[m]
+            for owner, blocks in ((2 * m, first), (2 * m + 1, second)):
+                at = 256 * (owner % 32) + 128 * (owner // 32)
+                out[:, at : at + 128] = blocks[m]
 
     @pl.when(core[0] == 0)
     def _():
@@ -224,7 +256,7 @@
         place(there, here)
 
 
-def call(kernel, name, out_shape, in_specs, args, scratch=(), flops=0):
+def call(kernel, out_shape, in_specs, args, scratch=(), flops=0):
     outs = jax.tree.map(lambda _: pl.BlockSpec(memory_space=pltpu.VMEM), out_shape)
     return pl.pallas_call(
         kernel,
@@ -232,13 +264,12 @@
         in_specs=in_specs,
         out_specs=outs,
         scratch_shapes=list(scratch),
-        name=name,
         compiler_params=pltpu.CompilerParams(vmem_limit_bytes=32 * 1024 * 1024),
         cost_estimate=pl.CostEstimate(flops=flops, bytes_accessed=0, transcendentals=0),
     )(*args)
 
 
-def local(inputs, cotangent, weights, momentum, keep_index):
+def step(inputs, cotangent, weights, momentum, keep_index):
     core = lax.axis_index("core").astype(jnp.int32)
     core_at = core.reshape(1)
     weight = weights[0]
@@ -247,8 +278,15 @@
     full = LAYERS * rows
     struct = jax.ShapeDtypeStruct
 
-    half = lax.dynamic_slice_in_dim(weight, core * (rows // 2), rows // 2, 0)
-    mine = a2a(half.reshape(rows // 2, LAYERS, cols).transpose(1, 0, 2), S)
+    half = call(
+        half_kernel,
+        struct((LAYERS, rows // 2, cols), BF),
+        [SCALAR, pl.BlockSpec(memory_space=pltpu.HBM)],
+        (core_at, weight),
+        [pltpu.SemaphoreType.DMA((LAYERS,))],
+        1000,
+    )
+    mine = a2a(half, S)
     other = swap_cores(mine)
     w = jnp.concatenate(
         [jnp.where(core == 0, mine, other), jnp.where(core == 0, other, mine)], axis=1
@@ -256,18 +294,20 @@
 
     proj = mm_nt(w, jnp.concatenate([inputs, cotangent], axis=0)).astype(BF).reshape(LAYERS, rows, 256)
     gram = mm_nt(w, w).astype(BF).reshape(LAYERS, rows, full)
-    packed = jnp.stack(
+    packed = (
         [gram[7, :, 256:]]
         + [jnp.concatenate([gram[l, :, :128], gram[7 - l, :, 256:384]], axis=1) for l in (1, 2)]
         + [gram[l, :, :256] for l in range(3, LAYERS)]
     )
-    payload = jnp.concatenate([proj, packed], axis=2)
-    got = jnp.sum(a2a(payload, S).astype(F32), axis=0).astype(BF)
-    got = a2a(jnp.broadcast_to(got[None], (LAYERS,) + got.shape), S)
+    chunks = [jnp.concatenate([proj[l], packed[l]], axis=1) for l in range(LAYERS)]
+    payload = jnp.stack([jnp.stack([chunks[x], chunks[x + 4]]) for x in range(4)])
+    part = jnp.sum(a2a(payload, "x").astype(F32), axis=0).astype(BF)
+    far = lax.ppermute(part, "zh", [(0, 1), (1, 0)])
+    got = (part.astype(F32) + far.astype(F32)).astype(BF)
+    got = a2a(jnp.broadcast_to(got[None], (4,) + got.shape), "x")
 
     grads = call(
         relay_kernel,
-        "relay",
         struct((LAYERS, rows, cols), BF),
         [SCALAR] + whole(5),
         (core_at, got, inputs, cotangent, mine, other),
@@ -277,31 +317,24 @@
     grad = a2a(grads, S)
 
     basis = dct_tables()
-    keep = keep_index[0, 0].reshape(64, 64)
-    keep = jnp.concatenate([keep, keep], axis=1)
-    coef, sent = call(
-        coef_kernel,
-        "coef",
-        (struct((rows, width), F32), struct((64, 128), F32)),
-        whole(5),
-        (grad, momentum[0, 0], keep, row_table(basis), col_table(basis.T, 4)),
-        (),
-        2 * 2048 * 768 * 256,
-    )
+    keep = keep_index[0, 0].reshape(32, 128)
+    values = struct((32, 128), F32)
+    tables = (row_table(basis), col_table(basis.T, 4))
+    flops = 2 * 2048 * 768 * 256
+    past = call(past_kernel, values, whole(4), (momentum[0, 0], keep) + tables, (), flops)
+    vals, sent = call(coef_kernel, (values, struct((64, 128), F32)), whole(5), (grad, past, keep) + tables, (), flops)
     seen = a2a(sent, DP)
     momentum_out = call(
         rest_kernel,
-        "rest",
         struct((rows, width), BF),
-        whole(4),
-        (coef, keep, row_table(basis.T), col_table(basis, 4)),
+        whole(6),
+        (vals, keep, momentum[0, 0], grad, row_table(basis.T), col_table(basis, 4)),
         (),
         2 * 2048 * 768 * 256 * 4,
     )
 
     spread = call(
         owner_kernel,
-        "owner",
         struct((32, 64, 128), BF),
         whole(3),
         (seen, row_table(basis.T), col_table(basis, 2)),
@@ -310,16 +343,14 @@
     )
     here = a2a(spread, CHIP)
     there = swap_cores(here)
-    update = call(
-        join_kernel, "join", struct((rows, width), BF), [SCALAR] + whole(2), (core_at, here, there), (), 1000
-    )
+    update = call(join_kernel, struct((rows, width), BF), [SCALAR] + whole(2), (core_at, here, there), (), 1000)
     return (momentum_out[None, None], update[None, None])
 
 
 def solution(mesh):
     fine = Mesh(mesh.devices.reshape(2, 4, 4, 8, 2), ("zh", "x", "zl", "y", "core"))
     return jax.shard_map(
-        local,
+        step,
         mesh=fine,
         in_specs=(
             P(DP, S),

time: 168 us -> 162 us (0.964)
  blocking collectives: 115 us -> 99.7 us
  waiting for transfers between devices: 14.5 us -> 25 us
  starting transfers between devices: 13.5 us -> 11.6 us
    all_to_all x5, blocking collectives: 115 us -> 99.7 us  [a2a(): return lax.all_to_all(value, axis, 0, 0, tiled=True)]
    ppermute x0 -> x1, waiting for transfers between devices: none -> 11.6 us  [step(): far = lax.ppermute(part, 'zh', [(0, 1), (1, 0)])]
    all_to_all x1, starting transfers between devices: 9.53 us -> 5.69 us  [a2a(): return lax.all_to_all(value, axis, 0, 0, tiled=True)]
    ppermute x0 -> x1, starting transfers between devices: none -> 1.92 us  [step(): far = lax.ppermute(part, 'zh', [(0, 1), (1, 0)])]
    pallas_call x5 -> x7, Pallas kernels: 17.1 us -> 18.3 us  [call(): pl.pallas_call(kernel, out_shape=out_shape, in_specs=in_specs, out_specs=...]
  transfers between devices with their start and end apart: 3 -> 4, of which waited for: 2 -> 3; matrix products, arithmetic and copies ran while one was open for 0% -> 0% of each run, Pallas kernels for 5% -> 5%
where the time goes in v3:
time: 162 us; the launch traced here: 159 us
  blocking collectives  99.7 us (62%)
  waiting for transfers between devices  25 us (15%)
  Pallas kernels  18.3 us (11%)
  starting transfers between devices  11.6 us (7%)
  local copies, waits for them, and re-layouts  1.74 us (1%)
    all_to_all x5, blocking collectives, a2a(): return lax.all_to_all(value, axis, 0, 0, tiled=True)  99.7 us
    pallas_call x7, Pallas kernels, call(): pl.pallas_call(kernel, out_shape=out_shape, in_specs=in_specs, out_specs=...  18.3 us
    ppermute x1, waiting for transfers between devices, step(): far = lax.ppermute(part, 'zh', [(0, 1), (1, 0)])  11.6 us
    all_to_all x1, waiting for transfers between devices, a2a(): return lax.all_to_all(value, axis, 0, 0, tiled=True)  11.5 us
    all_to_all x1, starting transfers between devices, a2a(): return lax.all_to_all(value, axis, 0, 0, tiled=True)  5.69 us
    ppermute x2, starting transfers between devices, swap_cores(): return lax.ppermute(value, 'core', [(0, 1), (1, 0)])  4 us
  transfers between devices with their start and end apart: 4, of which 3 were waited for; matrix products, arithmetic and copies ran while one was open for 0% of the time, Pallas kernels for 5%

profile of v3, /device:TPU:6, one launch (start us, length us, event | category | flops | bytes accessed | tf_op | source)
XLA Modules:
  0.0 158.9 jit_solution(8069299661907785868)
XLA Ops:
  0.6 1.2 copy-done
  1.9 0.2 shard_map.122
  2.1 24.6 %all_to_all.36.mine = bf16[8,32,1024]{2,1,0:T(8,128)(2,1)S(1)} all-to-all(bf16[8,32,1024]{2,1,0:T(8,128)(2,1)S(1)} %shard_map.122), channel_id=1, replica_groups=mesh['zh'=2,'x'=4,'zl'=4,'y'=8,'core'=2] {'zh','x'}, dimensions={0} | all-to-all | bytes 1048576 | tf_op jit(solution)/shard_map/all_to_all | solution.py:22
  26.7 1.9 %collective-permute-start = (bf16[8,32,1024]{2,1,0:T(8,128)(2,1)S(1)}, bf16[8,32,1024]{2,1,0:T(8,128)(2,1)S(1)}, u32[]{:S(2)}, u32[]{:S(2)}) collective-permute-start(bf16[8,32,1024]{2,1,0:T(8,128)(2,1)S(1)} %all_to_all.36.mine), channel_id=1, source_target_pairs={{0,1},{1,0},{2,3},{3,2},{4,5},{5,4},{6,7},{7,6},{8,9},{9,8},{10,11... | collective-permute-start | bytes 1572872 | tf_op jit(solution)/shard_map/ppermute | solution.py:26
  28.7 1.9 %collective-permute-done.other = bf16[8,32,1024]{2,1,0:T(8,128)(2,1)S(1)} collective-permute-done((bf16[8,32,1024]{2,1,0:T(8,128)(2,1)S(1)}, bf16[8,32,1024]{2,1,0:T(8,128)(2,1)S(1)}, u32[]{:S(2)}, u32[]{:S(2)}) %collective-permute-start) | collective-permute-done | bytes 524320 | tf_op jit(solution)/shard_map/ppermute | solution.py:26
  30.5 0.1 broadcast_select_fusion.1
  30.6 0.1 pad_maximum_fusion
  30.7 0.7 convolution_convert_fusion
  31.5 0.1 copy-done.1
  31.6 0.1 copy-done.2
  31.7 0.5 convolution_convert_fusion.1
  32.4 0.1 pad_maximum_fusion.1
  32.5 16.3 %all_to_all.37 = bf16[4,2,64,512]{3,2,1,0:T(8,128)(2,1)S(1)} all-to-all(bf16[4,2,64,512]{3,2,1,0:T(8,128)(2,1)S(1)} %pad_maximum_fusion.1), channel_id=1, replica_groups=mesh['zh'=2,'x'=4,'zl'=4,'y'=8,'core'=2] {'x'}, dimensions={0} | all-to-all | bytes 1048576 | tf_op jit(solution)/shard_map/all_to_all | solution.py:22
  48.8 0.1 reduce_sum.12
  48.8 1.9 %collective-permute-start.1 = (bf16[2,64,512]{2,1,0:T(8,128)(2,1)S(1)}, bf16[2,64,512]{2,1,0:T(8,128)(2,1)S(1)}, u32[]{:S(2)}, u32[]{:S(2)}) collective-permute-start(bf16[2,64,512]{2,1,0:T(8,128)(2,1)S(1)} %reduce_sum.12), channel_id=1, source_target_pairs={{0,256},{256,0},{1,257},{257,1},{2,258},{258,2},{3,259},{259,3},{4... | collective-permute-start | bytes 393224 | tf_op jit(solution)/shard_map/ppermute | solution.py:305
  50.8 11.6 %collective-permute-done.1 = bf16[2,64,512]{2,1,0:T(8,128)(2,1)S(1)} collective-permute-done((bf16[2,64,512]{2,1,0:T(8,128)(2,1)S(1)}, bf16[2,64,512]{2,1,0:T(8,128)(2,1)S(1)}, u32[]{:S(2)}, u32[]{:S(2)}) %collective-permute-start.1) | collective-permute-done | bytes 131104 | tf_op jit(solution)/shard_map/ppermute | solution.py:305
  62.5 10.5 %all_to_all.38.got = bf16[4,2,64,512]{3,2,1,0:T(8,128)(2,1)S(1)} all-to-all(bf16[4,2,64,512]{3,2,1,0:T(8,128)(2,1)S(1)} %broadcast_in_dim.12), channel_id=1, replica_groups=mesh['zh'=2,'x'=4,'zl'=4,'y'=8,'core'=2] {'x'}, dimensions={0} | all-to-all | bytes 1048576 | tf_op jit(solution)/shard_map/all_to_all | solution.py:22
  73.0 4.2 %shard_map.123 = bf16[8,64,1024]{2,1,0:T(8,128)(2,1)} custom-call(s32[1]{0:T(128)} %bitcast.core, bf16[4,2,64,512]{3,2,1,0:T(8,128)(2,1)S(1)} %all_to_all.38.got, bf16[128,1024]{1,0:T(8,128)(2,1)S(1)} %copy-done.2, bf16[128,1024]{1,0:T(8,128)(2,1)S(1)} %copy-done.1, bf16[8,32,1024]{2,1,0:T(8,128)(2,1)S(1)} %all_to_all.36.mine, ...), custom_call_target="tpu_custom_call" | custom-call | flops 805306368 | tf_op jit(solution)/shard_map/pallas_call | solution.py:261
  77.2 5.7 %all-to-all-start.3 = ((bf16[8,64,1024]{2,1,0:T(8,128)(2,1)}), bf16[8,64,1024]{2,1,0:T(8,128)(2,1)S(1)}, u32[]{:S(2)}, u32[]{:S(2)}) async-start(bf16[8,64,1024]{2,1,0:T(8,128)(2,1)} %shard_map.123), calls=%async_computation.3 | async-start | bytes 2097152 | tf_op jit(solution)/shard_map/all_to_all | solution.py:22
  82.9 0.1 copy.15
  83.0 0.1 reshape_squeeze.3.keep
  83.1 2.8 %shard_map.124.past = f32[32,128]{1,0:T(8,128)S(1)} custom-call(bf16[64,8192]{1,0:T(8,128)(2,1)S(1)} %bitcast.63, s32[32,128]{1,0:T(8,128)S(1)} %reshape_squeeze.3.keep, bf16[64,192]{1,0:T(8,128)(2,1)S(1)} %copy-done.8, bf16[768,256]{1,0:T(8,128)(2,1)S(1)} %copy-done.7), custom_call_target="tpu_custom_call" | custom-call | flops 805306368 | tf_op jit(solution)/shard_map/pallas_call | solution.py:261
  86.0 0.0 copy-start.3
  86.0 0.0 copy-start.4
  86.0 11.5 %all-to-all-done.3.grad = bf16[8,64,1024]{2,1,0:T(8,128)(2,1)S(1)} async-done(((bf16[8,64,1024]{2,1,0:T(8,128)(2,1)}), bf16[8,64,1024]{2,1,0:T(8,128)(2,1)S(1)}, u32[]{:S(2)}, u32[]{:S(2)}) %all-to-all-start.3) | async-done | bytes 1048608 | tf_op jit(solution)/shard_map/all_to_all | solution.py:22
  97.4 2.9 %shard_map.125 = (f32[32,128]{1,0:T(8,128)S(1)}, f32[64,128]{1,0:T(8,128)S(1)}) custom-call(bf16[8,64,1024]{2,1,0:T(8,128)(2,1)S(1)} %all-to-all-done.3.grad, f32[32,128]{1,0:T(8,128)S(1)} %shard_map.124.past, s32[32,128]{1,0:T(8,128)S(1)} %reshape_squeeze.3.keep, bf16[64,192]{1,0:T(8,128)(2,1)S(1)} %copy-done.8, bf16[768,256]{1,0:T(8,128)(2,1)S(1)} %copy-done.7), custom_call_target="tpu_custom_call" | custom-call | flops 805306368 | tf_op jit(solution)/shard_map/pallas_call | solution.py:261
  100.4 28.0 %all_to_all.39 = f32[64,1,128]{2,1,0:T(1,128)S(1)} all-to-all(f32[64,1,128]{2,1,0:T(1,128)S(1)} %bitcast.62), channel_id=1, replica_groups=mesh['zh'=2,'x'=4,'zl'=4,'y'=8,'core'=2] {'zl','y','core'}, dimensions={0} | all-to-all | bytes 65536 | tf_op jit(solution)/shard_map/all_to_all | solution.py:22
  128.3 1.0 shard_map.127
  129.4 20.4 %all_to_all.40.here = bf16[32,64,128]{2,1,0:T(8,128)(2,1)S(1)} all-to-all(bf16[32,64,128]{2,1,0:T(8,128)(2,1)S(1)} %shard_map.127), channel_id=1, replica_groups=mesh['zh'=2,'x'=4,'zl'=4,'y'=8,'core'=2] {'zl','y'}, dimensions={0} | all-to-all | bytes 1048576 | tf_op jit(solution)/shard_map/all_to_all | solution.py:22
  149.8 2.1 %collective-permute-start.2 = (bf16[32,64,128]{2,1,0:T(8,128)(2,1)S(1)}, bf16[32,64,128]{2,1,0:T(8,128)(2,1)S(1)}, u32[]{:S(2)}, u32[]{:S(2)}) collective-permute-start(bf16[32,64,128]{2,1,0:T(8,128)(2,1)S(1)} %all_to_all.40.here), channel_id=1, source_target_pairs={{0,1},{1,0},{2,3},{3,2},{4,5},{5,4},{6,7},{7,6},{8,9},{9,8},{10,11... | collective-permute-start | bytes 1572872 | tf_op jit(solution)/shard_map/ppermute | solution.py:26
  151.9 5.8 %shard_map.126 = bf16[64,8192]{1,0:T(8,128)(2,1)} custom-call(f32[32,128]{1,0:T(8,128)S(1)} %get-tuple-element.4.vals, s32[32,128]{1,0:T(8,128)S(1)} %reshape_squeeze.3.keep, bf16[64,8192]{1,0:T(8,128)(2,1)S(1)} %bitcast.64, bf16[8,64,1024]{2,1,0:T(8,128)(2,1)S(1)} %all-to-all-done.3.grad, bf16[64,192]{1,0:T(8,128)(2,1)S(1)} %copy-done.4, ...), custom_call_target="tpu_custom_call" | custom-call | flops 3221225472 | tf_op jit(solution)/shard_map/pallas_call | solution.py:261
  157.7 1.2 shard_map.128
  (29 shorter events, 0.3 us)
Async XLA Ops:
  0.6 1.2 copy-start
  26.7 3.8 %collective-permute-start = (bf16[8,32,1024]{2,1,0:T(8,128)(2,1)S(1)}, bf16[8,32,1024]{2,1,0:T(8,128)(2,1)S(1)}, u32[]{:S(2)}, u32[]{:S(2)}) collective-permute-start(bf16[8,32,1024]{2,1,0:T(8,128)(2,1)S(1)} %all_to_all.36.mine), channel_id=1, source_target_pairs={{0,1},{1,0},{2,3},{3,2},{4,5},{5,4},{6,7},{7,6},{8,9},{9,8},{10,11... | collective-permute-start | bytes 1572872 | tf_op jit(solution)/shard_map/ppermute | solution.py:26
  30.7 1.0 copy-start.1
  30.7 1.0 copy-start.2
  48.8 13.6 %collective-permute-start.1 = (bf16[2,64,512]{2,1,0:T(8,128)(2,1)S(1)}, bf16[2,64,512]{2,1,0:T(8,128)(2,1)S(1)}, u32[]{:S(2)}, u32[]{:S(2)}) collective-permute-start(bf16[2,64,512]{2,1,0:T(8,128)(2,1)S(1)} %reduce_sum.12), channel_id=1, source_target_pairs={{0,256},{256,0},{1,257},{257,1},{2,258},{258,2},{3,259},{259,3},{4... | collective-permute-start | bytes 393224 | tf_op jit(solution)/shard_map/ppermute | solution.py:305
  77.2 5.7 %copy-start.9 = (s32[1,1,128,32]{2,3,1,0:T(8,128)S(1)}, s32[1,1,128,32]{2,3,1,0:T(8,128)}, u32[]{:S(2)}) copy-start(s32[1,1,128,32]{2,3,1,0:T(8,128)} %param.15) | copy-start | bytes 49156
  77.2 5.9 %copy-start.5 = (bf16[1,1,64,8192]{3,2,1,0:T(8,128)(2,1)S(1)}, bf16[1,1,64,8192]{3,2,1,0:T(8,128)(2,1)}, u32[]{:S(2)}) copy-start(bf16[1,1,64,8192]{3,2,1,0:T(8,128)(2,1)} %param.14) | copy-start | bytes 3145732
  77.2 5.9 %copy-start.7 = (bf16[768,256]{1,0:T(8,128)(2,1)S(1)}, bf16[768,256]{1,0:T(8,128)(2,1)}, u32[]{:S(2)}) copy-start(bf16[768,256]{1,0:T(8,128)(2,1)} %constant.20.clone.col_t) | copy-start | bytes 1179652
  77.2 5.9 %copy-start.8 = (bf16[64,192]{1,0:T(8,128)(2,1)S(1)}, bf16[64,192]{1,0:T(8,128)(2,1)}, u32[]{:S(2)}) copy-start(bf16[64,192]{1,0:T(8,128)(2,1)} %constant.19.clone.row_t) | copy-start | bytes 73732
  77.2 20.2 %all-to-all-start.3 = ((bf16[8,64,1024]{2,1,0:T(8,128)(2,1)}), bf16[8,64,1024]{2,1,0:T(8,128)(2,1)S(1)}, u32[]{:S(2)}, u32[]{:S(2)}) async-start(bf16[8,64,1024]{2,1,0:T(8,128)(2,1)} %shard_map.123), calls=%async_computation.3 | async-start | bytes 2097152 | tf_op jit(solution)/shard_map/all_to_all | solution.py:22
  86.0 42.4 %copy-start.3 = (bf16[384,128]{1,0:T(8,128)(2,1)S(1)}, bf16[384,128]{1,0:T(8,128)(2,1)}, u32[]{:S(2)}) copy-start(bf16[384,128]{1,0:T(8,128)(2,1)} %constant.23.clone.col_t) | copy-start | bytes 294916
  86.0 42.4 %copy-start.4 = (bf16[64,192]{1,0:T(8,128)(2,1)S(1)}, bf16[64,192]{1,0:T(8,128)(2,1)}, u32[]{:S(2)}) copy-start(bf16[64,192]{1,0:T(8,128)(2,1)} %constant.21.clone.row_t) | copy-start | bytes 73732
  100.4 51.5 %copy-start.6 = (bf16[768,256]{1,0:T(8,128)(2,1)S(1)}, bf16[768,256]{1,0:T(8,128)(2,1)}, u32[]{:S(2)}) copy-start(bf16[768,256]{1,0:T(8,128)(2,1)} %constant.22.clone.col_t) | copy-start | bytes 1179652
  149.8 7.9 %collective-permute-start.2 = (bf16[32,64,128]{2,1,0:T(8,128)(2,1)S(1)}, bf16[32,64,128]{2,1,0:T(8,128)(2,1)S(1)}, u32[]{:S(2)}, u32[]{:S(2)}) collective-permute-start(bf16[32,64,128]{2,1,0:T(8,128)(2,1)S(1)} %all_to_all.40.here), channel_id=1, source_target_pairs={{0,1},{1,0},{2,3},{3,2},{4,5},{5,4},{6,7},{7,6},{8,9},{9,8},{10,11... | collective-permute-start | bytes 1572872 | tf_op jit(solution)/shard_map/ppermute | solution.py:26

commit v4 on v3

--- a/solution.py
+++ b/solution.py
@@ -84,8 +84,8 @@
     at_mine = pl.multiple_of(core[0] * 32, 32)
     at_other = pl.multiple_of(32 - core[0] * 32, 32)
     for l in range(LAYERS):
-        rhs[pl.ds(l * rows + at_mine, 32)] = mine[l]
-        rhs[pl.ds(l * rows + at_other, 32)] = other[l]
+        rhs[l * rows : l * rows + 32] = mine[l]
+        rhs[l * rows + 32 : l * rows + 64] = other[l]
     rhs[512:640] = g[...]
     rhs[640:768] = x[...]
     zero = jnp.zeros((rows, 128), BF)
@@ -138,7 +138,8 @@
         cols = slice(256 * n, 256 * n + 256)
         grads = mm(lhs, rhs[:, cols]).astype(BF)
         for l in range(LAYERS):
-            out[l, :, cols] = grads[rows * l : rows * l + rows]
+            out[l, pl.ds(at_mine, 32), cols] = grads[rows * l : rows * l + 32]
+            out[l, pl.ds(at_other, 32), cols] = grads[rows * l + 32 : rows * l + 64]
 
 
 def pick(z, row, col, lane):
@@ -162,7 +163,11 @@
     lane = lax.broadcasted_iota(jnp.int32, (1, 128), 1)
     for s in range(8):
         piece = field(s)
-        y = by_cols(jnp.concatenate([piece[:, 256 * q : 256 * q + 256] for q in range(4)], axis=0), col_t[...])
+        piece = jnp.concatenate([piece[:, 256 * q : 256 * q + 256] for q in range(4)], axis=0)
+        if piece.dtype == BF:
+            y = mm(jnp.concatenate([piece, piece], axis=1), col_t[256:768])
+        else:
+            y = by_cols(piece, col_t[...])
         for q in range(4):
             t = 4 * s + q
             z = by_rows(row_t[...], y[64 * q : 64 * q + 64])
@@ -175,7 +180,7 @@
 
 
 def coef_kernel(grad, past, keep, row_t, col_t, vals, sent):
-    choose(lambda s: grad[s].astype(F32), keep, row_t, col_t, vals)
+    choose(lambda s: grad[s], keep, row_t, col_t, vals)
     value = vals[...] + past[...]
     vals[...] = value
     where = keep[...].astype(F32)
@@ -288,9 +293,7 @@
     )
     mine = a2a(half, S)
     other = swap_cores(mine)
-    w = jnp.concatenate(
-        [jnp.where(core == 0, mine, other), jnp.where(core == 0, other, mine)], axis=1
-    ).reshape(full, cols)
+    w = jnp.concatenate([mine, other], axis=1).reshape(full, cols)
 
     proj = mm_nt(w, jnp.concatenate([inputs, cotangent], axis=0)).astype(BF).reshape(LAYERS, rows, 256)
     gram = mm_nt(w, w).astype(BF).reshape(LAYERS, rows, full)

time: 162 us -> 161 us (level)
  no operation moved by 1% of the time
where the time goes in v4:
time: 161 us; the launch traced here: 158 us
  blocking collectives  99.7 us (62%)
  waiting for transfers between devices  25 us (16%)
  Pallas kernels  17.8 us (11%)
  starting transfers between devices  11.6 us (7%)
  local copies, waits for them, and re-layouts  1.74 us (1%)
    all_to_all x5, blocking collectives, a2a(): return lax.all_to_all(value, axis, 0, 0, tiled=True)  99.7 us
    pallas_call x7, Pallas kernels, call(): pl.pallas_call(kernel, out_shape=out_shape, in_specs=in_specs, out_specs=...  17.8 us
    ppermute x1, waiting for transfers between devices, step(): far = lax.ppermute(part, 'zh', [(0, 1), (1, 0)])  11.6 us
    all_to_all x1, waiting for transfers between devices, a2a(): return lax.all_to_all(value, axis, 0, 0, tiled=True)  11.5 us
    all_to_all x1, starting transfers between devices, a2a(): return lax.all_to_all(value, axis, 0, 0, tiled=True)  5.68 us
    ppermute x2, starting transfers between devices, swap_cores(): return lax.ppermute(value, 'core', [(0, 1), (1, 0)])  4 us
  transfers between devices with their start and end apart: 4, of which 3 were waited for; matrix products, arithmetic and copies ran while one was open for 0% of the time, Pallas kernels for 5%

profile of v4, /device:TPU:6, one launch (start us, length us, event | category | flops | bytes accessed | tf_op | source)
XLA Modules:
  0.0 158.3 jit_solution(13939526395174806265)
XLA Ops:
  0.6 1.2 copy-done
  1.9 0.2 shard_map.122
  2.1 24.6 %all_to_all.36.mine = bf16[8,32,1024]{2,1,0:T(8,128)(2,1)S(1)} all-to-all(bf16[8,32,1024]{2,1,0:T(8,128)(2,1)S(1)} %shard_map.122), channel_id=1, replica_groups=mesh['zh'=2,'x'=4,'zl'=4,'y'=8,'core'=2] {'zh','x'}, dimensions={0} | all-to-all | bytes 1048576 | tf_op jit(solution)/shard_map/all_to_all | solution.py:22
  26.7 1.9 %collective-permute-start = (bf16[8,32,1024]{2,1,0:T(8,128)(2,1)S(1)}, bf16[8,32,1024]{2,1,0:T(8,128)(2,1)S(1)}, u32[]{:S(2)}, u32[]{:S(2)}) collective-permute-start(bf16[8,32,1024]{2,1,0:T(8,128)(2,1)S(1)} %all_to_all.36.mine), channel_id=1, source_target_pairs={{0,1},{1,0},{2,3},{3,2},{4,5},{5,4},{6,7},{7,6},{8,9},{9,8},{10,11... | collective-permute-start | bytes 1572872 | tf_op jit(solution)/shard_map/ppermute | solution.py:26
  28.7 1.9 %collective-permute-done.other = bf16[8,32,1024]{2,1,0:T(8,128)(2,1)S(1)} collective-permute-done((bf16[8,32,1024]{2,1,0:T(8,128)(2,1)S(1)}, bf16[8,32,1024]{2,1,0:T(8,128)(2,1)S(1)}, u32[]{:S(2)}, u32[]{:S(2)}) %collective-permute-start) | collective-permute-done | bytes 524320 | tf_op jit(solution)/shard_map/ppermute | solution.py:26
  30.5 0.1 pad_maximum_fusion
  30.6 0.0 copy-start.1
  30.7 0.7 convolution_convert_fusion
  31.5 0.1 copy-done.1
  31.6 0.1 copy-done.2
  31.7 0.5 convolution_convert_fusion.1
  32.4 0.1 pad_maximum_fusion.1
  32.4 16.3 %all_to_all.37 = bf16[4,2,64,512]{3,2,1,0:T(8,128)(2,1)S(1)} all-to-all(bf16[4,2,64,512]{3,2,1,0:T(8,128)(2,1)S(1)} %pad_maximum_fusion.1), channel_id=1, replica_groups=mesh['zh'=2,'x'=4,'zl'=4,'y'=8,'core'=2] {'x'}, dimensions={0} | all-to-all | bytes 1048576 | tf_op jit(solution)/shard_map/all_to_all | solution.py:22
  48.7 0.1 reduce_sum.12
  48.8 1.9 %collective-permute-start.1 = (bf16[2,64,512]{2,1,0:T(8,128)(2,1)S(1)}, bf16[2,64,512]{2,1,0:T(8,128)(2,1)S(1)}, u32[]{:S(2)}, u32[]{:S(2)}) collective-permute-start(bf16[2,64,512]{2,1,0:T(8,128)(2,1)S(1)} %reduce_sum.12), channel_id=1, source_target_pairs={{0,256},{256,0},{1,257},{257,1},{2,258},{258,2},{3,259},{259,3},{4... | collective-permute-start | bytes 393224 | tf_op jit(solution)/shard_map/ppermute | solution.py:308
  50.7 11.6 %collective-permute-done.1 = bf16[2,64,512]{2,1,0:T(8,128)(2,1)S(1)} collective-permute-done((bf16[2,64,512]{2,1,0:T(8,128)(2,1)S(1)}, bf16[2,64,512]{2,1,0:T(8,128)(2,1)S(1)}, u32[]{:S(2)}, u32[]{:S(2)}) %collective-permute-start.1) | collective-permute-done | bytes 131104 | tf_op jit(solution)/shard_map/ppermute | solution.py:308
  62.5 10.5 %all_to_all.38.got = bf16[4,2,64,512]{3,2,1,0:T(8,128)(2,1)S(1)} all-to-all(bf16[4,2,64,512]{3,2,1,0:T(8,128)(2,1)S(1)} %broadcast_in_dim.12), channel_id=1, replica_groups=mesh['zh'=2,'x'=4,'zl'=4,'y'=8,'core'=2] {'x'}, dimensions={0} | all-to-all | bytes 1048576 | tf_op jit(solution)/shard_map/all_to_all | solution.py:22
  72.9 4.3 %shard_map.123 = bf16[8,64,1024]{2,1,0:T(8,128)(2,1)} custom-call(s32[1]{0:T(128)} %bitcast.core, bf16[4,2,64,512]{3,2,1,0:T(8,128)(2,1)S(1)} %all_to_all.38.got, bf16[128,1024]{1,0:T(8,128)(2,1)S(1)} %copy-done.2, bf16[128,1024]{1,0:T(8,128)(2,1)S(1)} %copy-done.1, bf16[8,32,1024]{2,1,0:T(8,128)(2,1)S(1)} %all_to_all.36.mine, ...), custom_call_target="tpu_custom_call" | custom-call | flops 805306368 | tf_op jit(solution)/shard_map/pallas_call | solution.py:266
  77.2 5.7 %all-to-all-start.3 = ((bf16[8,64,1024]{2,1,0:T(8,128)(2,1)}), bf16[8,64,1024]{2,1,0:T(8,128)(2,1)S(1)}, u32[]{:S(2)}, u32[]{:S(2)}) async-start(bf16[8,64,1024]{2,1,0:T(8,128)(2,1)} %shard_map.123), calls=%async_computation.3 | async-start | bytes 2097152 | tf_op jit(solution)/shard_map/all_to_all | solution.py:22
  82.9 0.1 copy.15
  83.0 0.1 reshape_squeeze.3.keep
  83.1 2.8 %shard_map.124.past = f32[32,128]{1,0:T(8,128)S(1)} custom-call(bf16[64,8192]{1,0:T(8,128)(2,1)S(1)} %bitcast.63, s32[32,128]{1,0:T(8,128)S(1)} %reshape_squeeze.3.keep, bf16[64,192]{1,0:T(8,128)(2,1)S(1)} %copy-done.8, bf16[768,256]{1,0:T(8,128)(2,1)S(1)} %copy-done.7), custom_call_target="tpu_custom_call" | custom-call | flops 805306368 | tf_op jit(solution)/shard_map/pallas_call | solution.py:266
  86.0 0.0 copy-start.3
  86.0 0.0 copy-start.4
  86.0 11.5 %all-to-all-done.3.grad = bf16[8,64,1024]{2,1,0:T(8,128)(2,1)S(1)} async-done(((bf16[8,64,1024]{2,1,0:T(8,128)(2,1)}), bf16[8,64,1024]{2,1,0:T(8,128)(2,1)S(1)}, u32[]{:S(2)}, u32[]{:S(2)}) %all-to-all-start.3) | async-done | bytes 1048608 | tf_op jit(solution)/shard_map/all_to_all | solution.py:22
  97.4 2.4 %shard_map.125 = (f32[32,128]{1,0:T(8,128)S(1)}, f32[64,128]{1,0:T(8,128)S(1)}) custom-call(bf16[8,64,1024]{2,1,0:T(8,128)(2,1)S(1)} %all-to-all-done.3.grad, f32[32,128]{1,0:T(8,128)S(1)} %shard_map.124.past, s32[32,128]{1,0:T(8,128)S(1)} %reshape_squeeze.3.keep, bf16[64,192]{1,0:T(8,128)(2,1)S(1)} %copy-done.8, bf16[768,256]{1,0:T(8,128)(2,1)S(1)} %copy-done.7), custom_call_target="tpu_custom_call" | custom-call | flops 805306368 | tf_op jit(solution)/shard_map/pallas_call | solution.py:266
  99.8 28.0 %all_to_all.39 = f32[64,1,128]{2,1,0:T(1,128)S(1)} all-to-all(f32[64,1,128]{2,1,0:T(1,128)S(1)} %bitcast.62), channel_id=1, replica_groups=mesh['zh'=2,'x'=4,'zl'=4,'y'=8,'core'=2] {'zl','y','core'}, dimensions={0} | all-to-all | bytes 65536 | tf_op jit(solution)/shard_map/all_to_all | solution.py:22
  127.8 1.0 shard_map.127
  128.8 20.4 %all_to_all.40.here = bf16[32,64,128]{2,1,0:T(8,128)(2,1)S(1)} all-to-all(bf16[32,64,128]{2,1,0:T(8,128)(2,1)S(1)} %shard_map.127), channel_id=1, replica_groups=mesh['zh'=2,'x'=4,'zl'=4,'y'=8,'core'=2] {'zl','y'}, dimensions={0} | all-to-all | bytes 1048576 | tf_op jit(solution)/shard_map/all_to_all | solution.py:22
  149.2 2.1 %collective-permute-start.2 = (bf16[32,64,128]{2,1,0:T(8,128)(2,1)S(1)}, bf16[32,64,128]{2,1,0:T(8,128)(2,1)S(1)}, u32[]{:S(2)}, u32[]{:S(2)}) collective-permute-start(bf16[32,64,128]{2,1,0:T(8,128)(2,1)S(1)} %all_to_all.40.here), channel_id=1, source_target_pairs={{0,1},{1,0},{2,3},{3,2},{4,5},{5,4},{6,7},{7,6},{8,9},{9,8},{10,11... | collective-permute-start | bytes 1572872 | tf_op jit(solution)/shard_map/ppermute | solution.py:26
  151.4 5.8 %shard_map.126 = bf16[64,8192]{1,0:T(8,128)(2,1)} custom-call(f32[32,128]{1,0:T(8,128)S(1)} %get-tuple-element.4.vals, s32[32,128]{1,0:T(8,128)S(1)} %reshape_squeeze.3.keep, bf16[64,8192]{1,0:T(8,128)(2,1)S(1)} %bitcast.64, bf16[8,64,1024]{2,1,0:T(8,128)(2,1)S(1)} %all-to-all-done.3.grad, bf16[64,192]{1,0:T(8,128)(2,1)S(1)} %copy-done.4, ...), custom_call_target="tpu_custom_call" | custom-call | flops 3221225472 | tf_op jit(solution)/shard_map/pallas_call | solution.py:266
  157.2 1.2 shard_map.128
  (28 shorter events, 0.3 us)
Async XLA Ops:
  0.6 1.2 copy-start
  26.7 3.8 %collective-permute-start = (bf16[8,32,1024]{2,1,0:T(8,128)(2,1)S(1)}, bf16[8,32,1024]{2,1,0:T(8,128)(2,1)S(1)}, u32[]{:S(2)}, u32[]{:S(2)}) collective-permute-start(bf16[8,32,1024]{2,1,0:T(8,128)(2,1)S(1)} %all_to_all.36.mine), channel_id=1, source_target_pairs={{0,1},{1,0},{2,3},{3,2},{4,5},{5,4},{6,7},{7,6},{8,9},{9,8},{10,11... | collective-permute-start | bytes 1572872 | tf_op jit(solution)/shard_map/ppermute | solution.py:26
  30.6 1.0 copy-start.1
  30.7 1.0 copy-start.2
  48.8 13.6 %collective-permute-start.1 = (bf16[2,64,512]{2,1,0:T(8,128)(2,1)S(1)}, bf16[2,64,512]{2,1,0:T(8,128)(2,1)S(1)}, u32[]{:S(2)}, u32[]{:S(2)}) collective-permute-start(bf16[2,64,512]{2,1,0:T(8,128)(2,1)S(1)} %reduce_sum.12), channel_id=1, source_target_pairs={{0,256},{256,0},{1,257},{257,1},{2,258},{258,2},{3,259},{259,3},{4... | collective-permute-start | bytes 393224 | tf_op jit(solution)/shard_map/ppermute | solution.py:308
  77.2 5.7 %copy-start.9 = (s32[1,1,128,32]{2,3,1,0:T(8,128)S(1)}, s32[1,1,128,32]{2,3,1,0:T(8,128)}, u32[]{:S(2)}) copy-start(s32[1,1,128,32]{2,3,1,0:T(8,128)} %param.15) | copy-start | bytes 49156
  77.2 5.9 %copy-start.5 = (bf16[1,1,64,8192]{3,2,1,0:T(8,128)(2,1)S(1)}, bf16[1,1,64,8192]{3,2,1,0:T(8,128)(2,1)}, u32[]{:S(2)}) copy-start(bf16[1,1,64,8192]{3,2,1,0:T(8,128)(2,1)} %param.14) | copy-start | bytes 3145732
  77.2 5.9 %copy-start.7 = (bf16[768,256]{1,0:T(8,128)(2,1)S(1)}, bf16[768,256]{1,0:T(8,128)(2,1)}, u32[]{:S(2)}) copy-start(bf16[768,256]{1,0:T(8,128)(2,1)} %constant.18.clone.col_t) | copy-start | bytes 1179652
  77.2 5.9 %copy-start.8 = (bf16[64,192]{1,0:T(8,128)(2,1)S(1)}, bf16[64,192]{1,0:T(8,128)(2,1)}, u32[]{:S(2)}) copy-start(bf16[64,192]{1,0:T(8,128)(2,1)} %constant.17.clone.row_t) | copy-start | bytes 73732
  77.2 20.2 %all-to-all-start.3 = ((bf16[8,64,1024]{2,1,0:T(8,128)(2,1)}), bf16[8,64,1024]{2,1,0:T(8,128)(2,1)S(1)}, u32[]{:S(2)}, u32[]{:S(2)}) async-start(bf16[8,64,1024]{2,1,0:T(8,128)(2,1)} %shard_map.123), calls=%async_computation.3 | async-start | bytes 2097152 | tf_op jit(solution)/shard_map/all_to_all | solution.py:22
  86.0 41.8 %copy-start.3 = (bf16[384,128]{1,0:T(8,128)(2,1)S(1)}, bf16[384,128]{1,0:T(8,128)(2,1)}, u32[]{:S(2)}) copy-start(bf16[384,128]{1,0:T(8,128)(2,1)} %constant.21.clone.col_t) | copy-start | bytes 294916
  86.0 41.8 %copy-start.4 = (bf16[64,192]{1,0:T(8,128)(2,1)S(1)}, bf16[64,192]{1,0:T(8,128)(2,1)}, u32[]{:S(2)}) copy-start(bf16[64,192]{1,0:T(8,128)(2,1)} %constant.19.clone.row_t) | copy-start | bytes 73732
  99.8 51.5 %copy-start.6 = (bf16[768,256]{1,0:T(8,128)(2,1)S(1)}, bf16[768,256]{1,0:T(8,128)(2,1)}, u32[]{:S(2)}) copy-start(bf16[768,256]{1,0:T(8,128)(2,1)} %constant.20.clone.col_t) | copy-start | bytes 1179652
  149.2 7.9 %collective-permute-start.2 = (bf16[32,64,128]{2,1,0:T(8,128)(2,1)S(1)}, bf16[32,64,128]{2,1,0:T(8,128)(2,1)S(1)}, u32[]{:S(2)}, u32[]{:S(2)}) collective-permute-start(bf16[32,64,128]{2,1,0:T(8,128)(2,1)S(1)} %all_to_all.40.here), channel_id=1, source_target_pairs={{0,1},{1,0},{2,3},{3,2},{4,5},{5,4},{6,7},{7,6},{8,9},{9,8},{10,11... | collective-permute-start | bytes 1572872 | tf_op jit(solution)/shard_map/ppermute | solution.py:26
